TPU v7x, 32 devices: a whole 2x2x4 slice. The times are simulated.
32 devices in a mesh: node: 8 (over z, x), expert: 4 (over y, core).
Axes of the slice: x: 2, y: 2, z: 4, core: 2. Of those that a mesh axis runs over, the one named last changes fastest.
Arguments:
- tokens: bfloat16 [16384, 1024], P(('node', 'expert')), may hold values from -6 to 6
- queries: bfloat16 [16384, 1024], P(('node', 'expert')), may hold values from -6 to 6
- keys: bfloat16 [16384, 1024], P(('node', 'expert')), may hold values from -6 to 6
- values: bfloat16 [16384, 1024], P(('node', 'expert')), may hold values from -12 to 12
- neighbours: int32 [128, 8], P(('node', 'expert')), may hold values from 0 to 127, as said below
- live_bits: int32 [128, 8], P(('node', 'expert')), may hold values from 0 to 1, as said below
- out_proj: bfloat16 [1024, 1024], replicated, may hold values from -0.1875 to 0.1875
- norm_gain: float32 [1024], replicated, may hold values from 0.5 to 1.5
- router: bfloat16 [1024, 32], replicated, may hold values from -0.1875 to 0.1875
- expert: int32 [16384], P(('node', 'expert')), may hold values from 0 to 31, as said below
- slot: int32 [16384], P(('node', 'expert')), may hold values from 0 to 31, as said below
- w_up: bfloat16 [32, 1024, 4096], P(('node', 'expert')), may hold values from -0.1875 to 0.1875
- w_down: bfloat16 [32, 4096, 1024], P(('node', 'expert')), may hold values from -0.09375 to 0.09375
Outputs:
- layer_out: bfloat16 [16384, 1024], P(('node', 'expert'))
Inputs may be any that keep to these rules, and one draw needn't show every extreme that they name: Tile g is held by device g // 4 in node-major order. neighbours[g, 0] is g itself; every listed tile is held by g's device or by the device one step before or after it along node with the same expert index (wrapping around); entry 1 is always one step before and entry 2 one step after. `live_bits`: entry 0 of every row is 1. Within the 512 tokens of one device, no two tokens share both expert and slot; some expert takes all 32 slots of every device. See expert: pairs (expert, slot) are distinct within one device's tokens.
All inputs are finite; a program needn't handle non-finite values.
Results may differ from a plain program's by a relative error of at most 0.0049.
Values may be sent and summed in bfloat16 or wider, within the bound.
No kernel may reach another device: no remote copies, remote signals or barrier semaphores. Data moves between devices by JAX's collectives and lax.ppermute only.
A program may use at most 192 MiB of HBM per device.

v0:
```python
import jax
import jax.numpy as jnp
from jax import lax
from jax.sharding import PartitionSpec as P

D = 1024
HEADS = 16
HEAD_DIM = 64
TILE = 128
NB = 8


score_scale = 0.125


def extended(shard, sides, width):
    for axis, dim in sides:
        size, length = (lax.axis_size(axis), shard.shape[dim])
        up = [(i, (i + 1) % size) for i in range(size)]
        down = [(j, i) for i, j in up]
        last = lax.slice_in_dim(shard, length - width, length, axis=dim)
        leading = lax.slice_in_dim(shard, 0, width, axis=dim)
        before = lax.ppermute(last, axis, up)
        after = lax.ppermute(leading, axis, down)
        shard = jnp.concatenate([before, shard, after], axis=dim)
    return shard


def shards(
    tokens,
    queries,
    keys,
    values,
    neighbours,
    live_bits,
    out_proj,
    norm_gain,
    router,
    expert,
    slot,
    w_up,
    w_down,
):
    tok_dev = tokens.shape[0]
    tiles_dev = tok_dev // TILE
    experts = router.shape[1]
    cap = 2 * tok_dev // experts
    both = jnp.concatenate([keys, values], axis=1)
    widened = extended(both, (("node", 0),), tok_dev)
    window_tiles = widened.reshape(3 * tiles_dev, TILE, 2 * D)
    my_node = lax.axis_index("node")
    node_count = lax.axis_size("node")
    column_count = lax.axis_size("expert")
    owner_node = neighbours // tiles_dev // column_count
    offset = (owner_node - my_node + node_count) % node_count
    block_of = jnp.where(offset == 0, 1, jnp.where(offset == 1, 2, 0))
    position = block_of * tiles_dev + neighbours % tiles_dev
    gathered = window_tiles[position]
    near_keys = gathered[..., :D].reshape(tiles_dev, NB * TILE, HEADS, HEAD_DIM)
    near_values = gathered[..., D:].reshape(tiles_dev, NB * TILE, HEADS, HEAD_DIM)
    query_tiles = queries.reshape(tiles_dev, TILE, HEADS, HEAD_DIM)
    scores = (
        jnp.einsum("tqhd,tkhd->thqk", query_tiles, near_keys, preferred_element_type=jnp.float32)
        * score_scale
    )
    visible = jnp.repeat(live_bits, TILE, axis=1) > 0
    masked = jnp.where(visible[:, None, None, :], scores, -jnp.inf)
    peak = jnp.max(masked, axis=-1, keepdims=True)
    weights = jnp.exp(masked - peak)
    weights = (weights / jnp.sum(weights, axis=-1, keepdims=True)).astype(jnp.bfloat16)
    mixed = jnp.einsum("thqk,tkhd->tqhd", weights, near_values, preferred_element_type=jnp.float32)
    attn = mixed.reshape(tok_dev, D).astype(jnp.bfloat16)
    hidden = tokens.astype(jnp.float32) + jnp.dot(
        attn, out_proj, preferred_element_type=jnp.float32
    )
    spread = jnp.mean(hidden * hidden, axis=-1, keepdims=True)
    normed = (hidden * lax.rsqrt(spread + 1e-06) * norm_gain[None, :]).astype(jnp.bfloat16)
    logits = jnp.dot(normed, router, preferred_element_type=jnp.float32)
    columns = lax.iota(jnp.int32, experts)
    chosen = jnp.sum(jnp.where(columns[None, :] == expert[:, None], logits, 0.0), axis=-1)
    gate = jax.nn.sigmoid(chosen)
    slot_cell = expert * cap + slot
    one_hot = (lax.iota(jnp.int32, experts * cap)[:, None] == slot_cell[None, :]).astype(
        jnp.bfloat16
    )
    outgoing = jnp.dot(one_hot, normed, preferred_element_type=jnp.float32).astype(jnp.bfloat16)
    up_matrix = w_up[0]
    down_matrix = w_down[0]
    block = lax.all_to_all(
        outgoing.reshape(experts, 1, cap, D),
        ("node", "expert"),
        split_axis=0,
        concat_axis=1,
        tiled=True,
    )
    token_rows = block.reshape(-1, D)
    lifted = jnp.dot(token_rows, up_matrix, preferred_element_type=jnp.float32)
    lifted = jax.nn.gelu(lifted, approximate=True).astype(jnp.bfloat16)
    result = jnp.dot(lifted, down_matrix, preferred_element_type=jnp.float32).astype(jnp.bfloat16)
    returned = lax.all_to_all(
        result.reshape(block.shape), ("node", "expert"), split_axis=1, concat_axis=0, tiled=True
    )
    flat_back = returned.reshape(experts * cap, D)
    expert_out = jnp.einsum("ct,cd->td", one_hot, flat_back, preferred_element_type=jnp.float32)
    layer_out = hidden + gate[:, None] * expert_out
    return layer_out.astype(jnp.bfloat16)


def solution(mesh):
    in_specs = (
        P(("node", "expert"), None),
        P(("node", "expert"), None),
        P(("node", "expert"), None),
        P(("node", "expert"), None),
        P(("node", "expert"), None),
        P(("node", "expert"), None),
        P(),
        P(),
        P(),
        P(("node", "expert")),
        P(("node", "expert")),
        P(("node", "expert"), None, None),
        P(("node", "expert"), None, None),
    )
    out_specs = P(("node", "expert"), None)
    return jax.shard_map(shards, mesh=mesh, in_specs=in_specs, out_specs=out_specs, check_vma=False)
```

profile of v0, /device:TPU:0, one launch (start us, length us, event | category | flops | bytes accessed | tf_op | source)
XLA Modules:
  0.0 354.1 jit_solution(12946120193367616058)
XLA Ops:
  0.0 2.5 constant_dynamic-update-slice_fusion.1
  2.5 2.3 constant_dynamic-update-slice_fusion
  4.8 6.0 %collective-permute-start.1 = (bf16[512,2048]{1,0:T(8,128)(2,1)}, bf16[512,2048]{1,0:T(8,128)(2,1)}, u32[]{:S(2)}, u32[]{:S(2)}) collective-permute-start(bf16[512,2048]{1,0:T(8,128)(2,1)} %constant_dynamic-update-slice_fusion), channel_id=1, source_target_pairs={{4,0},{8,4},{12,8},{16,12},{20,16},{24,20},{28,24},{0,28},{5,1},{9... | collective-permute-start | bytes 6291464 | tf_op jit(solution)/shard_map/ppermute | solution.py:24
  10.8 0.0 collective-permute-start
  10.8 0.7 compare_select_fusion
  11.5 0.1 reshape.71
  11.6 0.7 broadcast_compare_fusion
  12.3 0.1 broadcast_bitcast_fusion
  12.3 4.0 %reshape.79 = bf16[4,128,16,64]{3,2,1,0:T(8,128)(2,1)} reshape(bf16[512,1024]{1,0:T(8,128)(2,1)} %param.14) | data formatting | bytes 2097152 | tf_op jit(solution)/shard_map/reshape | solution.py:61
  16.4 82.2 %collective-permute-done.1 = bf16[512,2048]{1,0:T(8,128)(2,1)} collective-permute-done((bf16[512,2048]{1,0:T(8,128)(2,1)}, bf16[512,2048]{1,0:T(8,128)(2,1)}, u32[]{:S(2)}, u32[]{:S(2)}) %collective-permute-start.1) | collective-permute-done | bytes 2097184 | tf_op jit(solution)/shard_map/ppermute | solution.py:24
  98.6 0.2 collective-permute-done
  98.8 5.9 %pad_maximum_fusion = bf16[1536,2048]{1,0:T(8,128)(2,1)} fusion(bf16[512,2048]{1,0:T(8,128)(2,1)} %collective-permute-done.1, bf16[512,2048]{1,0:T(8,128)(2,1)} %constant_dynamic-update-slice_fusion, bf16[512,2048]{1,0:T(8,128)(2,1)} %collective-permute-done), kind=kLoop, calls=%fused_computation.28 | loop fusion | flops 18874368 | bytes 12582912 | tf_op jit(solution)/shard_map/concatenate | solution.py:25
  104.7 10.1 %gather_fusion = bf16[32,128,2048]{2,1,0:T(8,128)(2,1)} fusion(bf16[12,128,2048]{2,1,0:T(8,128)(2,1)} %bitcast.64, s32[1024]{0:T(1024)S(1)} %pad_clamp_fusion), kind=kCustom, calls=%fused_computation | custom fusion | bytes 33554560 | tf_op jit(solution)/shard_map/gather | solution.py:58
  114.7 11.9 %fusion.66 = (bf16[4,8,128,1024]{3,2,1,0:T(8,128)(2,1)}, bf16[4,8,128,1024]{3,2,1,0:T(8,128)(2,1)}) fusion(bf16[4,8,128,2048]{3,2,1,0:T(8,128)(2,1)} %bitcast.65), kind=kLoop, calls=%fused_computation.88 | loop fusion | bytes 33554432 | tf_op jit(solution)/shard_map/slice | solution.py:59
  126.6 12.3 %copy.22 = bf16[4,8,128,1024]{2,1,3,0:T(8,128)(2,1)} copy(bf16[4,8,128,1024]{3,2,1,0:T(8,128)(2,1)} %get-tuple-element.6) | data formatting | bytes 16777216 | tf_op jit(solution)/shard_map/slice | solution.py:60
  138.9 13.3 %reshape.62 = bf16[4,1024,16,64]{1,3,2,0:T(8,128)(2,1)} reshape(bf16[4,8,128,1024]{2,1,3,0:T(8,128)(2,1)} %copy.22) | data formatting | bytes 16777216 | tf_op jit(solution)/shard_map/reshape | solution.py:60
  152.2 12.3 %copy.23 = bf16[4,8,128,1024]{2,1,3,0:T(8,128)(2,1)} copy(bf16[4,8,128,1024]{3,2,1,0:T(8,128)(2,1)} %get-tuple-element.5) | data formatting | bytes 16777216 | tf_op jit(solution)/shard_map/slice | solution.py:59
  164.6 13.3 %reshape.63 = bf16[4,1024,16,64]{1,3,2,0:T(8,128)(2,1)} reshape(bf16[4,8,128,1024]{2,1,3,0:T(8,128)(2,1)} %copy.23) | data formatting | bytes 16777216 | tf_op jit(solution)/shard_map/reshape | solution.py:59
  177.8 18.8 %fusion.67 = (f32[4,16,128]{2,1,0:T(8,128)S(1)}, f32[4,16,128,1024]{2,3,1,0:T(8,128)}) fusion(pred[4,1024]{1,0:T(4,128)(4,1)S(1)} %bitcast.69, bf16[4,1024,16,64]{1,3,2,0:T(8,128)(2,1)} %reshape.63, bf16[4,128,16,64]{3,2,1,0:T(8,128)(2,1)} %reshape.79), kind=kOutput, calls=%fused_computation.89 | convolution fusion | flops 1107297280 | bytes 43028480 | tf_op jit(solution)/shard_map/sub | solution.py:69
  196.6 14.6 %fusion.47 = bf16[4,128,16,64]{1,3,2,0:T(8,128)(2,1)S(1)} fusion(bf16[4,1024,16,64]{1,3,2,0:T(8,128)(2,1)} %reshape.62, f32[4,16,128,1024]{2,3,1,0:T(8,128)} %get-tuple-element.8, f32[4,16,128]{2,1,0:T(8,128)S(1)} %get-tuple-element.7), kind=kOutput, calls=%fused_computation.43 | convolution fusion | flops 1091043328 | bytes 43024384 | tf_op jit(solution)/shard_map/thqk,tkhd->tqhd/dot_general | solution.py:71
  211.3 0.0 copy-start.6
  211.3 0.9 copy.27
  212.2 2.6 multiply_reduce_fusion
  214.8 1.3 copy-done.2
  216.1 1.4 fusion.38
  217.5 54.6 %all_to_all.8 = bf16[32,1,32,1024]{3,2,1,0:T(8,128)(2,1)S(1)} all-to-all(bf16[32,1,32,1024]{3,2,1,0:T(8,128)(2,1)S(1)} %bitcast.68), channel_id=1, replica_groups=mesh['node'=8,'expert'=4] {'node','expert'}, dimensions={0} | all-to-all | bytes 4194304 | tf_op jit(solution)/shard_map/all_to_all | solution.py:89
  272.1 25.0 %fusion.29 = bf16[1024,1024]{1,0:T(8,128)(2,1)} fusion(bf16[1,4096,1024]{2,1,0:T(8,128)(2,1)} %param.25, bf16[1024,1024]{1,0:T(8,128)(2,1)S(1)} %bitcast.67, bf16[1,1024,4096]{2,1,0:T(8,128)(2,1)} %param.24), kind=kOutput, calls=%fused_computation.37 | convolution fusion | flops 17218666496 | bytes 20971520 | tf_op jit(solution)/shard_map/dot_general | solution.py:99
  297.1 3.8 %all-to-all-start.1 = ((bf16[1,32,32,1024]{3,2,0,1:T(8,128)(2,1)}), bf16[1,32,32,1024]{3,2,0,1:T(8,128)(2,1)}, u32[]{:S(2)}, u32[]{:S(2)}) async-start(bf16[1,32,32,1024]{3,2,0,1:T(8,128)(2,1)} %bitcast.10), calls=%async_computation.1 | async-start | bytes 4194304 | tf_op jit(solution)/shard_map/all_to_all | solution.py:100
  300.9 0.0 copy-start.1
  301.0 2.2 fusion.48
  303.2 46.4 %all-to-all-done.1 = bf16[1,32,32,1024]{3,2,0,1:T(8,128)(2,1)} async-done(((bf16[1,32,32,1024]{3,2,0,1:T(8,128)(2,1)}), bf16[1,32,32,1024]{3,2,0,1:T(8,128)(2,1)}, u32[]{:S(2)}, u32[]{:S(2)}) %all-to-all-start.1) | async-done | bytes 2097184 | tf_op jit(solution)/shard_map/all_to_all | solution.py:100
  349.6 4.5 %add_convert_fusion = bf16[512,1024]{1,0:T(8,128)(2,1)} fusion(f32[512,1024]{1,0:T(8,128)} %copy-done.2, bf16[1024,1024]{1,0:T(8,128)(2,1)} %bitcast.11, s32[512]{0:T(512)S(1)} %multiply_add_fusion, f32[512]{0:T(512)S(1)} %add_divide_fusion), kind=kOutput, calls=%fused_computation.30 | convolution fusion | flops 1075838976 | bytes 5246976 | tf_op jit(solution)/shard_map/ct,cd->td/dot_general | solution.py:104
  (18 shorter events, 0.1 us)
Async XLA Ops:
  0.0 212.2 %copy-start = (bf16[1024,1024]{1,0:T(8,128)(2,1)S(1)}, bf16[1024,1024]{1,0:T(8,128)(2,1)}, u32[]{:S(2)}) copy-start(bf16[1024,1024]{1,0:T(8,128)(2,1)} %param.19) | copy-start | bytes 6291460
  0.0 16.4 %copy-start.7 = (s32[512]{0:T(512)S(1)}, s32[512]{0:T(512)}, u32[]{:S(2)}) copy-start(s32[512]{0:T(512)} %param.23) | copy-start | bytes 6148
  0.0 16.4 %copy-start.4 = (s32[512]{0:T(512)S(1)}, s32[512]{0:T(512)}, u32[]{:S(2)}) copy-start(s32[512]{0:T(512)} %param.22) | copy-start | bytes 6148
  4.8 93.9 %collective-permute-start.1 = (bf16[512,2048]{1,0:T(8,128)(2,1)}, bf16[512,2048]{1,0:T(8,128)(2,1)}, u32[]{:S(2)}, u32[]{:S(2)}) collective-permute-start(bf16[512,2048]{1,0:T(8,128)(2,1)} %constant_dynamic-update-slice_fusion), channel_id=1, source_target_pairs={{4,0},{8,4},{12,8},{16,12},{20,16},{24,20},{28,24},{0,28},{5,1},{9... | collective-permute-start | bytes 6291464 | tf_op jit(solution)/shard_map/ppermute | solution.py:24
  10.8 88.0 %collective-permute-start = (bf16[512,2048]{1,0:T(8,128)(2,1)}, bf16[512,2048]{1,0:T(8,128)(2,1)}, u32[]{:S(2)}, u32[]{:S(2)}) collective-permute-start(bf16[512,2048]{1,0:T(8,128)(2,1)} %constant_dynamic-update-slice_fusion), channel_id=1, source_target_pairs={{0,4},{4,8},{8,12},{12,16},{16,20},{20,24},{24,28},{28,0},{1,5},{5... | collective-permute-start | bytes 6291464 | tf_op jit(solution)/shard_map/ppermute | solution.py:23
  211.3 4.9 %copy-start.6 = (f32[1024]{0:T(1024)S(1)}, f32[1024]{0:T(1024)}, u32[]{:S(2)}) copy-start(f32[1024]{0:T(1024)} %param.20) | copy-start | bytes 12292
  214.8 1.3 copy-start.2
  272.1 28.8 %copy-start.3 = (bf16[1024,32]{0,1:T(8,128)(2,1)S(1)}, bf16[1024,32]{0,1:T(8,128)(2,1)}, u32[]{:S(2)}) copy-start(bf16[1024,32]{0,1:T(8,128)(2,1)} %param.21) | copy-start | bytes 196612
  272.1 28.8 %copy-start.5 = (s32[512]{0:T(512)S(1)}, s32[512]{0:T(512)}, u32[]{:S(2)}) copy-start(s32[512]{0:T(512)} %param.22) | copy-start | bytes 6148
  297.1 52.5 %all-to-all-start.1 = ((bf16[1,32,32,1024]{3,2,0,1:T(8,128)(2,1)}), bf16[1,32,32,1024]{3,2,0,1:T(8,128)(2,1)}, u32[]{:S(2)}, u32[]{:S(2)}) async-start(bf16[1,32,32,1024]{3,2,0,1:T(8,128)(2,1)} %bitcast.10), calls=%async_computation.1 | async-start | bytes 4194304 | tf_op jit(solution)/shard_map/all_to_all | solution.py:100
  300.9 53.2 %copy-start.1 = (bf16[1024,1024]{1,0:T(8,128)(2,1)S(1)}, bf16[1024,1024]{1,0:T(8,128)(2,1)}, u32[]{:S(2)}) copy-start(bf16[1024,1024]{1,0:T(8,128)(2,1)} %param.19) | copy-start | bytes 6291460
where the time goes:
time: 356 us; the launch traced here: 354 us
  waiting for transfers between devices  129 us (36%)
  local copies, waits for them, and re-layouts  84.3 us (24%)
  matrix products  69.1 us (19%)
  blocking collectives  54.6 us (15%)
  starting transfers between devices  9.8 us (3%)
  other arithmetic  7.34 us (2%)
    ppermute x1, waiting for transfers between devices, extended(): after = lax.ppermute(leading, axis, down)  82.2 us
    all_to_all x1, blocking collectives, shards(): lax.all_to_all(outgoing.reshape(experts, 1, cap, D), ('node', 'expert'),...  54.6 us
    all_to_all x1, waiting for transfers between devices, shards(): lax.all_to_all(result.reshape(block.shape), ('node', 'expert'), split_axi...  46.4 us
    dot_general x1, matrix products, shards(): jnp.dot(lifted, down_matrix, preferred_element_type=jnp.float32)  25 us
    slice x2, local copies, waits for them, and re-layouts, shards(): near_keys = gathered[..., :D].reshape(tiles_dev, NB * TILE, HEADS, HEAD_DIM)  24.2 us
    sub x1, matrix products, shards(): weights = jnp.exp(masked - peak)  18.8 us
    dot_general x1, matrix products, shards(): jnp.einsum('thqk,tkhd->tqhd', weights, near_values, preferred_element_typ...  14.6 us
    reshape x1, local copies, waits for them, and re-layouts, shards(): gathered[..., D:].reshape(tiles_dev, NB * TILE, HEADS, HEAD_DIM)  13.3 us
  transfers between devices with their start and end apart: 3, of which 3 were waited for; matrix products, arithmetic and copies ran while one was open for 2% of the time, Pallas kernels for 0%

commit v1 on v0

v1 whole, which is shorter than its diff:
```python
import jax
import jax.numpy as jnp
from jax import lax
from jax.experimental import pallas as pl
from jax.experimental.pallas import tpu as pltpu
from jax.sharding import PartitionSpec as P


D = 1024
HEAD_DIM = 64
TILE = 128
NB = 8
PAIR = 2 * HEAD_DIM

score_scale = 0.125
SCALE2 = score_scale * 1.4426950408889634
CHUNK_PAIRS = (2, 2, 2, 2)


def attend_kernel(pos_ref, live_ref, q_ref, own_ref, near_ref, far_ref, o_ref, kv, sems):
    tiles = q_ref.shape[0] // TILE
    pairs = q_ref.shape[1] // PAIR
    nb = pos_ref.shape[1]
    copies = [
        pltpu.make_async_copy(ref, kv.at[pl.ds(2 * tiles * i, 2 * tiles)], sems.at[i])
        for i, ref in enumerate((own_ref, near_ref, far_ref))
    ]
    for copy in copies:
        copy.start()
    for copy in copies:
        copy.wait()
    first = lax.broadcasted_iota(jnp.int32, (TILE, PAIR), 1) < HEAD_DIM

    def unit(index):
        t = index // pairs
        p = index - t * pairs
        rows = pl.ds(pl.multiple_of(t * TILE, TILE), TILE)
        cols = pl.ds(pl.multiple_of(p * PAIR, PAIR), PAIR)
        q = q_ref[rows, cols]
        zero = jnp.zeros_like(q)
        two_heads = jnp.concatenate(
            [jnp.where(first, q, zero), jnp.where(first, zero, q)], axis=0
        )
        scores, biases, peak = [], [], None
        for j in range(nb):
            key = kv[pos_ref[t, j], :, cols]
            score = lax.dot_general(
                key, two_heads, (((1,), (1,)), ((), ())), preferred_element_type=jnp.float32
            )
            bias = jnp.where(live_ref[t, j] > 0, jnp.float32(0.0), jnp.float32(-jnp.inf))
            top = jnp.max(score, axis=0, keepdims=True) + bias
            peak = top if peak is None else jnp.maximum(peak, top)
            scores.append(score)
            biases.append(bias)
        base = peak * SCALE2
        total, out = None, None
        for j in range(0, nb, 2):
            powers = []
            for i in (j, j + 1):
                power = jnp.exp2(scores[i] * SCALE2 - (base - biases[i]))
                part = jnp.sum(power, axis=0, keepdims=True)
                total = part if total is None else total + part
                powers.append(power.astype(jnp.bfloat16))
            value = jnp.concatenate(
                [kv[pos_ref[t, i] + tiles, :, cols] for i in (j, j + 1)], axis=0
            )
            mixed = lax.dot_general(
                value,
                jnp.concatenate(powers, axis=0),
                (((0,), (0,)), ((), ())),
                preferred_element_type=jnp.float32,
            )
            out = mixed if out is None else out + mixed
        inverse = 1.0 / total
        both = jnp.concatenate(
            [
                out[:HEAD_DIM, :TILE] * inverse[:, :TILE],
                out[HEAD_DIM:, TILE:] * inverse[:, TILE:],
            ],
            axis=0,
        )
        o_ref[rows, cols] = both.T.astype(jnp.bfloat16)

    def step(i, carry):
        unit(2 * i)
        unit(2 * i + 1)
        return carry

    lax.fori_loop(0, tiles * pairs // 2, step, 0)


def attend(queries, first_col, blocks, position, live_bits):
    tok, width = queries.shape[0], blocks[0].shape[1]
    tiles = tok // TILE
    blocks = [block.reshape(2 * tiles, TILE, width) for block in blocks]
    query = lax.slice_in_dim(queries, first_col, first_col + width, axis=1)
    return pl.pallas_call(
        attend_kernel,
        out_shape=jax.ShapeDtypeStruct((tok, width), jnp.bfloat16),
        grid_spec=pltpu.PrefetchScalarGridSpec(
            num_scalar_prefetch=2,
            grid=(1,),
            in_specs=[pl.BlockSpec((tok, width), lambda i, *_: (0, 0))]
            + [pl.BlockSpec(memory_space=pl.ANY)] * 3,
            out_specs=pl.BlockSpec((tok, width), lambda i, *_: (0, 0)),
            scratch_shapes=[
                pltpu.VMEM((6 * tiles, TILE, width), jnp.bfloat16),
                pltpu.SemaphoreType.DMA((3,)),
            ],
        ),
        compiler_params=pltpu.CompilerParams(vmem_limit_bytes=40 << 20),
        cost_estimate=pl.CostEstimate(
            flops=4 * tok * NB * TILE * width * 2,
            transcendentals=tok * NB * TILE * width // HEAD_DIM,
            bytes_accessed=8 * tok * width * 2,
        ),
        name="attend",
    )(position, live_bits, query, *blocks)


def layer(
    tokens,
    queries,
    keys,
    values,
    neighbours,
    live_bits,
    out_proj,
    norm_gain,
    router,
    expert,
    slot,
    w_up,
    w_down,
):
    tok_dev = tokens.shape[0]
    tiles_dev = tok_dev // TILE
    experts = router.shape[1]
    cap = 2 * tok_dev // experts
    my_node = lax.axis_index("node")
    node_count = lax.axis_size("node")
    column_count = lax.axis_size("expert")
    swap = [(i, i ^ 1) for i in range(node_count)]
    onward = [(i, (i + 2 - 4 * (i % 2)) % node_count) for i in range(node_count)]
    is_odd = my_node % 2
    owner_node = neighbours // tiles_dev // column_count
    offset = (owner_node - my_node + node_count) % node_count
    near_offset = jnp.where(is_odd == 1, node_count - 1, 1)
    block_of = jnp.where(offset == 0, 0, jnp.where(offset == near_offset, 1, 2))
    position = block_of * (2 * tiles_dev) + neighbours % tiles_dev
    mixed = []
    col = 0
    for pairs in CHUNK_PAIRS:
        width = pairs * PAIR
        own = jnp.concatenate([keys[:, col : col + width], values[:, col : col + width]], axis=0)
        near = lax.ppermute(own, "node", swap)
        far = lax.ppermute(near, "node", onward)
        mixed.append(attend(queries, col, (own, near, far), position, live_bits))
        col += width
    attn = jnp.concatenate(mixed, axis=1)
    hidden = tokens.astype(jnp.float32) + jnp.dot(
        attn, out_proj, preferred_element_type=jnp.float32
    )
    spread = jnp.mean(hidden * hidden, axis=-1, keepdims=True)
    normed = (hidden * lax.rsqrt(spread + 1e-06) * norm_gain[None, :]).astype(jnp.bfloat16)
    logits = jnp.dot(normed, router, preferred_element_type=jnp.float32)
    columns = lax.iota(jnp.int32, experts)
    chosen = jnp.sum(jnp.where(columns[None, :] == expert[:, None], logits, 0.0), axis=-1)
    gate = jax.nn.sigmoid(chosen)
    slot_cell = expert * cap + slot
    one_hot = (lax.iota(jnp.int32, experts * cap)[:, None] == slot_cell[None, :]).astype(
        jnp.bfloat16
    )
    outgoing = jnp.dot(one_hot, normed, preferred_element_type=jnp.float32).astype(jnp.bfloat16)
    up_matrix = w_up[0]
    down_matrix = w_down[0]
    block = lax.all_to_all(
        outgoing.reshape(experts, 1, cap, D),
        ("node", "expert"),
        split_axis=0,
        concat_axis=1,
        tiled=True,
    )
    token_rows = block.reshape(-1, D)
    lifted = jnp.dot(token_rows, up_matrix, preferred_element_type=jnp.float32)
    lifted = jax.nn.gelu(lifted, approximate=True).astype(jnp.bfloat16)
    result = jnp.dot(lifted, down_matrix, preferred_element_type=jnp.float32).astype(jnp.bfloat16)
    returned = lax.all_to_all(
        result.reshape(block.shape), ("node", "expert"), split_axis=1, concat_axis=0, tiled=True
    )
    flat_back = returned.reshape(experts * cap, D)
    expert_out = jnp.einsum("ct,cd->td", one_hot, flat_back, preferred_element_type=jnp.float32)
    layer_out = hidden + gate[:, None] * expert_out
    return layer_out.astype(jnp.bfloat16)


def solution(mesh):
    in_specs = (
        P(("node", "expert"), None),
        P(("node", "expert"), None),
        P(("node", "expert"), None),
        P(("node", "expert"), None),
        P(("node", "expert"), None),
        P(("node", "expert"), None),
        P(),
        P(),
        P(),
        P(("node", "expert")),
        P(("node", "expert")),
        P(("node", "expert"), None, None),
        P(("node", "expert"), None, None),
    )
    out_specs = P(("node", "expert"), None)
    return jax.shard_map(layer, mesh=mesh, in_specs=in_specs, out_specs=out_specs, check_vma=False)
```

time: 356 us -> 221 us (0.62)
  local copies, waits for them, and re-layouts: 84.3 us -> 4.8 us
  waiting for transfers between devices: 129 us -> 82.6 us
  matrix products: 69.1 us -> 34.9 us
  Pallas kernels: 0 us -> 27.3 us
  starting transfers between devices: 9.8 us -> 17.2 us
  other arithmetic: 7.34 us -> 0.19 us
    ppermute x2 -> x8, waiting for transfers between devices: 82.3 us -> 36 us  [the longest x4 36 us: layer(): near = lax.ppermute(own, 'node', swap)]
    slice x3 -> x2, local copies, waits for them, and re-layouts: 36.5 us -> 2.74 us  [the longest x1 1.82 us: layer(): keys[:, col:col + width]]
    reshape x3 -> x0, local copies, waits for them, and re-layouts: 30.6 us -> none  [the longest x1 13.3 us: shards(): gathered[..., D:].reshape(tiles_dev, NB * TILE, HEADS, HEAD_DIM)]
    pallas_call x0 -> x4, Pallas kernels: none -> 27.3 us  [attend(): pl.pallas_call(attend_kernel, out_shape=jax.ShapeDtypeStruct((tok, width)...]
    sub x1 -> x0, matrix products: 18.8 us -> none  [shards(): weights = jnp.exp(masked - peak)]
    dot_general x6 -> x5, matrix products: 50.4 us -> 34.9 us  [the longest x1 25.6 us: layer(): jnp.dot(lifted, down_matrix, preferred_element_type=jnp.float32)]
    gather x1 -> x0, local copies, waits for them, and re-layouts: 10.1 us -> none  [shards(): gathered = window_tiles[position]]
    ppermute x2 -> x8, starting transfers between devices: 6.01 us -> 13.4 us  [the longest x4 8.14 us: layer(): far = lax.ppermute(near, 'node', onward)]
  transfers between devices with their start and end apart: 3 -> 9, of which waited for: 3 -> 5; matrix products, arithmetic and copies ran while one was open for 2% -> 1% of each run, Pallas kernels for 0% -> 9%
where the time goes in v1:
time: 221 us
  waiting for transfers between devices  82.6 us (37%)
  blocking collectives  53.4 us (24%)
  matrix products  34.9 us (16%)
  Pallas kernels  27.3 us (12%)
  starting transfers between devices  17.2 us (8%)
  local copies, waits for them, and re-layouts  4.8 us (2%)
    all_to_all x1, blocking collectives, layer(): lax.all_to_all(outgoing.reshape(experts, 1, cap, D), ('node', 'expert'),...  53.4 us
    all_to_all x1, waiting for transfers between devices, layer(): lax.all_to_all(result.reshape(block.shape), ('node', 'expert'), split_axi...  46.6 us
    ppermute x4, waiting for transfers between devices, layer(): near = lax.ppermute(own, 'node', swap)  36 us
    pallas_call x4, Pallas kernels, attend(): pl.pallas_call(attend_kernel, out_shape=jax.ShapeDtypeStruct((tok, width)...  27.3 us
    dot_general x1, matrix products, layer(): jnp.dot(lifted, down_matrix, preferred_element_type=jnp.float32)  25.6 us
    ppermute x4, starting transfers between devices, layer(): far = lax.ppermute(near, 'node', onward)  8.14 us
    ppermute x4, starting transfers between devices, layer(): near = lax.ppermute(own, 'node', swap)  5.27 us
    dot_general x1, matrix products, layer(): jnp.einsum('ct,cd->td', one_hot, flat_back, preferred_element_type=jnp.fl...  4.49 us
  transfers between devices with their start and end apart: 9, of which 5 were waited for; matrix products, arithmetic and copies ran while one was open for 1% of the time, Pallas kernels for 9%

profile of v1, /device:TPU:0, one launch (start us, length us, event | category | flops | bytes accessed | tf_op | source)
XLA Modules:
  0.0 220.7 jit_solution(226364627560725404)
XLA Ops:
  0.0 1.8 fusion.50
  1.8 0.0 copy-start.10
  1.9 3.0 %collective-permute-start.4 = (bf16[1024,256]{1,0:T(8,128)(2,1)S(1)}, bf16[1024,256]{1,0:T(8,128)(2,1)}, u32[]{:S(2)}, u32[]{:S(2)}) collective-permute-start(bf16[1024,256]{1,0:T(8,128)(2,1)S(1)} %pad_maximum_fusion.2), channel_id=1, source_target_pairs={{0,4},{4,0},{8,12},{12,8},{16,20},{20,16},{24,28},{28,24},{1,5},{5... | collective-permute-start | bytes 1572872 | tf_op jit(solution)/shard_map/ppermute | solution.py:156
  5.0 0.1 collective-permute-start.6
  5.1 0.0 copy-start.14
  5.1 2.0 collective-permute-start.2
  7.2 0.1 collective-permute-start
  7.3 10.5 %collective-permute-done.4 = bf16[1024,256]{1,0:T(8,128)(2,1)} collective-permute-done((bf16[1024,256]{1,0:T(8,128)(2,1)S(1)}, bf16[1024,256]{1,0:T(8,128)(2,1)}, u32[]{:S(2)}, u32[]{:S(2)}) %collective-permute-start.4) | collective-permute-done | bytes 524320 | tf_op jit(solution)/shard_map/ppermute | solution.py:156
  17.8 2.1 collective-permute-start.5
  19.9 0.9 fusion.52
  20.8 8.2 %collective-permute-done.6 = bf16[1024,256]{1,0:T(8,128)(2,1)} collective-permute-done((bf16[1024,256]{1,0:T(8,128)(2,1)S(1)}, bf16[1024,256]{1,0:T(8,128)(2,1)}, u32[]{:S(2)}, u32[]{:S(2)}) %collective-permute-start.6) | collective-permute-done | bytes 524320 | tf_op jit(solution)/shard_map/ppermute | solution.py:156
  29.0 2.1 collective-permute-start.7
  31.1 9.1 %collective-permute-done.2 = bf16[1024,256]{1,0:T(8,128)(2,1)} collective-permute-done((bf16[1024,256]{1,0:T(8,128)(2,1)S(1)}, bf16[1024,256]{1,0:T(8,128)(2,1)}, u32[]{:S(2)}, u32[]{:S(2)}) %collective-permute-start.2) | collective-permute-done | bytes 524320 | tf_op jit(solution)/shard_map/ppermute | solution.py:156
  40.3 2.1 collective-permute-start.3
  42.4 0.0 copy-start.2
  42.4 8.2 %collective-permute-done = bf16[1024,256]{1,0:T(8,128)(2,1)} collective-permute-done((bf16[1024,256]{1,0:T(8,128)(2,1)S(1)}, bf16[1024,256]{1,0:T(8,128)(2,1)}, u32[]{:S(2)}, u32[]{:S(2)}) %collective-permute-start) | collective-permute-done | bytes 524320 | tf_op jit(solution)/shard_map/ppermute | solution.py:156
  50.7 1.8 collective-permute-start.1
  52.5 1.0 copy-done.4
  53.6 0.9 copy-done.7
  54.5 6.9 %attend.6 = bf16[512,256]{1,0:T(8,128)(2,1)S(1)} custom-call(s32[4,8]{1,0:T(4,128)S(1)} %fusion.42.pos_ref, s32[4,8]{1,0:T(4,128)S(1)} %copy-done.8, bf16[512,256]{1,0:T(8,128)(2,1)S(1)} %copy-done.7, bf16[8,128,256]{2,1,0:T(8,128)(2,1)S(1)} %bitcast.39, bf16[8,128,256]{2,1,0:T(8,128)(2,1)} %bitcast.7.near_ref, bf16[8,128,256]{2,1,0:T(8,128)(2,1)} %bitcast.8.far_ref), custom_call_target="tpu_custom_call" | custom-call | flops 1073741824 | bytes 2097152 | tf_op jit(solution)/shard_map/attend/pallas_call | solution.py:97
  61.4 6.9 %attend.7 = bf16[512,256]{1,0:T(8,128)(2,1)S(1)} custom-call(s32[4,8]{1,0:T(4,128)S(1)} %fusion.42.pos_ref, s32[4,8]{1,0:T(4,128)S(1)} %copy-done.8, bf16[512,256]{1,0:T(8,128)(2,1)S(1)} %copy-done.6, bf16[8,128,256]{2,1,0:T(8,128)(2,1)S(1)} %bitcast.38, bf16[8,128,256]{2,1,0:T(8,128)(2,1)} %bitcast.10.near_ref, bf16[8,128,256]{2,1,0:T(8,128)(2,1)} %bitcast.11.far_ref), custom_call_target="tpu_custom_call" | custom-call | flops 1073741824 | bytes 2097152 | tf_op jit(solution)/shard_map/attend/pallas_call | solution.py:97
  68.3 6.9 %attend.5 = bf16[512,256]{1,0:T(8,128)(2,1)S(1)} custom-call(s32[4,8]{1,0:T(4,128)S(1)} %fusion.42.pos_ref, s32[4,8]{1,0:T(4,128)S(1)} %copy-done.8, bf16[512,256]{1,0:T(8,128)(2,1)S(1)} %copy-done.5, bf16[8,128,256]{2,1,0:T(8,128)(2,1)S(1)} %bitcast.37, bf16[8,128,256]{2,1,0:T(8,128)(2,1)} %bitcast.4.near_ref, bf16[8,128,256]{2,1,0:T(8,128)(2,1)} %bitcast.5.far_ref), custom_call_target="tpu_custom_call" | custom-call | flops 1073741824 | bytes 2097152 | tf_op jit(solution)/shard_map/attend/pallas_call | solution.py:97
  75.3 6.7 %attend.4 = bf16[512,256]{1,0:T(8,128)(2,1)S(1)} custom-call(s32[4,8]{1,0:T(4,128)S(1)} %fusion.42.pos_ref, s32[4,8]{1,0:T(4,128)S(1)} %copy-done.8, bf16[512,256]{1,0:T(8,128)(2,1)S(1)} %get-tuple-element.13.q_ref, bf16[8,128,256]{2,1,0:T(8,128)(2,1)S(1)} %bitcast.36, bf16[8,128,256]{2,1,0:T(8,128)(2,1)} %bitcast.1.near_ref, bf16[8,128,256]{2,1,0:T(8,128)(2,1)S(1)} %bitcast.40), custom_call_target="tpu_custom_call" | custom-call | flops 1073741824 | bytes 2097152 | tf_op jit(solution)/shard_map/attend/pallas_call | solution.py:97
  82.0 0.0 copy-start.13
  82.0 1.4 multiply_reduce_fusion
  83.4 1.4 fusion.27
  84.8 53.4 %all_to_all.8 = bf16[32,1,32,1024]{3,2,1,0:T(8,128)(2,1)} all-to-all(bf16[32,1,32,1024]{3,2,1,0:T(8,128)(2,1)S(1)} %bitcast.43), channel_id=1, replica_groups=mesh['node'=8,'expert'=4] {'node','expert'}, dimensions={0} | all-to-all | bytes 4194304 | tf_op jit(solution)/shard_map/all_to_all | solution.py:177
  138.2 25.6 %fusion.18 = bf16[1024,1024]{1,0:T(8,128)(2,1)} fusion(bf16[1,4096,1024]{2,1,0:T(8,128)(2,1)} %param.25, bf16[1024,1024]{1,0:T(8,128)(2,1)} %bitcast.42, bf16[1,1024,4096]{2,1,0:T(8,128)(2,1)} %param.24), kind=kOutput, calls=%fused_computation.23 | convolution fusion | flops 17218666496 | bytes 20971520 | tf_op jit(solution)/shard_map/dot_general | solution.py:187
  163.8 3.8 %all-to-all-start.1 = ((bf16[1,32,32,1024]{3,2,0,1:T(8,128)(2,1)}), bf16[1,32,32,1024]{3,2,0,1:T(8,128)(2,1)}, u32[]{:S(2)}, u32[]{:S(2)}) async-start(bf16[1,32,32,1024]{3,2,0,1:T(8,128)(2,1)} %bitcast.41), calls=%async_computation.1 | async-start | bytes 4194304 | tf_op jit(solution)/shard_map/all_to_all | solution.py:188
  167.6 2.1 fusion.28
  169.7 46.6 %all-to-all-done.1 = bf16[1,32,32,1024]{3,2,0,1:T(8,128)(2,1)} async-done(((bf16[1,32,32,1024]{3,2,0,1:T(8,128)(2,1)}), bf16[1,32,32,1024]{3,2,0,1:T(8,128)(2,1)}, u32[]{:S(2)}, u32[]{:S(2)}) %all-to-all-start.1) | async-done | bytes 2097184 | tf_op jit(solution)/shard_map/all_to_all | solution.py:188
  216.3 4.5 %add_convert_fusion = bf16[512,1024]{1,0:T(8,128)(2,1)} fusion(f32[512,1024]{1,0:T(8,128)} %copy-done.9, bf16[1024,1024]{1,0:T(8,128)(2,1)} %bitcast.19, s32[512]{0:T(512)S(1)} %multiply_add_fusion, f32[512]{0:T(512)S(1)} %add_divide_fusion), kind=kOutput, calls=%fused_computation.16 | convolution fusion | flops 1075838976 | bytes 5246976 | tf_op jit(solution)/shard_map/ct,cd->td/dot_general | solution.py:192
  (40 shorter events, 0.3 us)
Async XLA Ops:
  0.0 82.0 %copy-start = (bf16[1024,1024]{1,0:T(8,128)(2,1)S(1)}, bf16[1024,1024]{1,0:T(8,128)(2,1)}, u32[]{:S(2)}) copy-start(bf16[1024,1024]{1,0:T(8,128)(2,1)} %param.19) | copy-start | bytes 6291460
  1.8 18.1 %copy-start.10 = (bf16[512,1024]{1,0:T(8,128)(2,1)S(1)}, bf16[512,1024]{1,0:T(8,128)(2,1)}, u32[]{:S(2)}) copy-start(bf16[512,1024]{1,0:T(8,128)(2,1)} %param.14) | copy-start | bytes 3145732
  1.9 19.0 %copy-start.3 = (bf16[1024,256]{1,0:T(8,128)(2,1)}, bf16[1024,256]{1,0:T(8,128)(2,1)S(1)}, u32[]{:S(2)}) copy-start(bf16[1024,256]{1,0:T(8,128)(2,1)S(1)} %pad_maximum_fusion.2) | copy-start | bytes 1572868
  1.9 15.9 %collective-permute-start.4 = (bf16[1024,256]{1,0:T(8,128)(2,1)S(1)}, bf16[1024,256]{1,0:T(8,128)(2,1)}, u32[]{:S(2)}, u32[]{:S(2)}) collective-permute-start(bf16[1024,256]{1,0:T(8,128)(2,1)S(1)} %pad_maximum_fusion.2), channel_id=1, source_target_pairs={{0,4},{4,0},{8,12},{12,8},{16,20},{20,16},{24,28},{28,24},{1,5},{5... | collective-permute-start | bytes 1572872 | tf_op jit(solution)/shard_map/ppermute | solution.py:156
  5.0 15.9 %copy-start.1 = (bf16[1024,256]{1,0:T(8,128)(2,1)}, bf16[1024,256]{1,0:T(8,128)(2,1)S(1)}, u32[]{:S(2)}) copy-start(bf16[1024,256]{1,0:T(8,128)(2,1)S(1)} %pad_maximum_fusion.3) | copy-start | bytes 1572868
  5.0 24.1 %collective-permute-start.6 = (bf16[1024,256]{1,0:T(8,128)(2,1)S(1)}, bf16[1024,256]{1,0:T(8,128)(2,1)}, u32[]{:S(2)}, u32[]{:S(2)}) collective-permute-start(bf16[1024,256]{1,0:T(8,128)(2,1)S(1)} %pad_maximum_fusion.3), channel_id=1, source_target_pairs={{0,4},{4,0},{8,12},{12,8},{16,20},{20,16},{24,28},{28,24},{1,5},{5... | collective-permute-start | bytes 1572872 | tf_op jit(solution)/shard_map/ppermute | solution.py:156
  5.1 37.3 %copy-start.12 = (s32[512]{0:T(512)S(1)}, s32[512]{0:T(512)}, u32[]{:S(2)}) copy-start(s32[512]{0:T(512)} %param.22) | copy-start | bytes 6148
  5.1 37.3 %copy-start.14 = (s32[512]{0:T(512)S(1)}, s32[512]{0:T(512)}, u32[]{:S(2)}) copy-start(s32[512]{0:T(512)} %param.23) | copy-start | bytes 6148
  5.1 47.4 %copy-start.15 = (s32[4,8]{1,0:T(4,128)S(1)}, s32[4,8]{1,0:T(4,128)}, u32[]{:S(2)}) copy-start(s32[4,8]{1,0:T(4,128)} %param.17) | copy-start | bytes 388
  5.1 47.4 %copy-start.8 = (s32[4,8]{1,0:T(4,128)S(1)}, s32[4,8]{1,0:T(4,128)}, u32[]{:S(2)}) copy-start(s32[4,8]{1,0:T(4,128)} %live_ref.7) | copy-start | bytes 388
  5.1 35.1 %collective-permute-start.2 = (bf16[1024,256]{1,0:T(8,128)(2,1)S(1)}, bf16[1024,256]{1,0:T(8,128)(2,1)}, u32[]{:S(2)}, u32[]{:S(2)}) collective-permute-start(bf16[1024,256]{1,0:T(8,128)(2,1)S(1)} %pad_maximum_fusion.1), channel_id=1, source_target_pairs={{0,4},{4,0},{8,12},{12,8},{16,20},{20,16},{24,28},{28,24},{1,5},{5... | collective-permute-start | bytes 1572872 | tf_op jit(solution)/shard_map/ppermute | solution.py:156
  7.2 43.4 %collective-permute-start = (bf16[1024,256]{1,0:T(8,128)(2,1)S(1)}, bf16[1024,256]{1,0:T(8,128)(2,1)}, u32[]{:S(2)}, u32[]{:S(2)}) collective-permute-start(bf16[1024,256]{1,0:T(8,128)(2,1)S(1)} %pad_maximum_fusion), channel_id=1, source_target_pairs={{0,4},{4,0},{8,12},{12,8},{16,20},{20,16},{24,28},{28,24},{1,5},{5... | collective-permute-start | bytes 1572872 | tf_op jit(solution)/shard_map/ppermute | solution.py:156
  17.8 34.7 %collective-permute-start.5 = (bf16[1024,256]{1,0:T(8,128)(2,1)}, bf16[1024,256]{1,0:T(8,128)(2,1)}, u32[]{:S(2)}, u32[]{:S(2)}) collective-permute-start(bf16[1024,256]{1,0:T(8,128)(2,1)} %collective-permute-done.4), channel_id=1, source_target_pairs={{0,8},{4,28},{8,16},{12,4},{16,24},{20,12},{24,0},{28,20},{1,9},{5... | collective-permute-start | bytes 1572872 | tf_op jit(solution)/shard_map/ppermute | solution.py:157
  29.0 32.4 %collective-permute-start.7 = (bf16[1024,256]{1,0:T(8,128)(2,1)}, bf16[1024,256]{1,0:T(8,128)(2,1)}, u32[]{:S(2)}, u32[]{:S(2)}) collective-permute-start(bf16[1024,256]{1,0:T(8,128)(2,1)} %collective-permute-done.6), channel_id=1, source_target_pairs={{0,8},{4,28},{8,16},{12,4},{16,24},{20,12},{24,0},{28,20},{1,9},{5... | collective-permute-start | bytes 1572872 | tf_op jit(solution)/shard_map/ppermute | solution.py:157
  40.3 28.1 %collective-permute-start.3 = (bf16[1024,256]{1,0:T(8,128)(2,1)}, bf16[1024,256]{1,0:T(8,128)(2,1)}, u32[]{:S(2)}, u32[]{:S(2)}) collective-permute-start(bf16[1024,256]{1,0:T(8,128)(2,1)} %collective-permute-done.2), channel_id=1, source_target_pairs={{0,8},{4,28},{8,16},{12,4},{16,24},{20,12},{24,0},{28,20},{1,9},{5... | collective-permute-start | bytes 1572872 | tf_op jit(solution)/shard_map/ppermute | solution.py:157
  42.4 19.0 %copy-start.2 = (bf16[1024,256]{1,0:T(8,128)(2,1)S(1)}, bf16[1024,256]{1,0:T(8,128)(2,1)}, u32[]{:S(2)}) copy-start(bf16[1024,256]{1,0:T(8,128)(2,1)} %copy-done.1) | copy-start | bytes 1572868
  50.7 24.6 %collective-permute-start.1 = (bf16[1024,256]{1,0:T(8,128)(2,1)}, bf16[1024,256]{1,0:T(8,128)(2,1)S(1)}, u32[]{:S(2)}, u32[]{:S(2)}) collective-permute-start(bf16[1024,256]{1,0:T(8,128)(2,1)} %collective-permute-done), channel_id=1, source_target_pairs={{0,8},{4,28},{8,16},{12,4},{16,24},{20,12},{24,0},{28,20},{1,9},{5... | collective-permute-start | bytes 1572872 | tf_op jit(solution)/shard_map/ppermute | solution.py:157
  52.5 1.0 copy-start.4
  53.6 0.9 copy-start.7
  54.5 6.9 %copy-start.6 = (bf16[512,256]{1,0:T(8,128)(2,1)S(1)}, bf16[512,256]{1,0:T(8,128)(2,1)}, u32[]{:S(2)}) copy-start(bf16[512,256]{1,0:T(8,128)(2,1)} %get-tuple-element.15.q_ref) | copy-start | bytes 786436
  61.4 6.9 %copy-start.5 = (bf16[512,256]{1,0:T(8,128)(2,1)S(1)}, bf16[512,256]{1,0:T(8,128)(2,1)}, u32[]{:S(2)}) copy-start(bf16[512,256]{1,0:T(8,128)(2,1)} %get-tuple-element.14.q_ref) | copy-start | bytes 786436
  75.2 6.8 %copy-start.16 = (bf16[512,1024]{1,0:T(8,128)(2,1)S(1)}, bf16[512,1024]{1,0:T(8,128)(2,1)}, u32[]{:S(2)}) copy-start(bf16[512,1024]{1,0:T(8,128)(2,1)} %param.13) | copy-start | bytes 3145732
  82.0 1.4 copy-start.13
  83.4 1.4 copy-start.9
  163.8 3.8 %copy-start.11 = (bf16[1024,32]{0,1:T(8,128)(2,1)S(1)}, bf16[1024,32]{0,1:T(8,128)(2,1)}, u32[]{:S(2)}) copy-start(bf16[1024,32]{0,1:T(8,128)(2,1)} %param.21) | copy-start | bytes 196612
  163.8 52.5 %all-to-all-start.1 = ((bf16[1,32,32,1024]{3,2,0,1:T(8,128)(2,1)}), bf16[1,32,32,1024]{3,2,0,1:T(8,128)(2,1)}, u32[]{:S(2)}, u32[]{:S(2)}) async-start(bf16[1,32,32,1024]{3,2,0,1:T(8,128)(2,1)} %bitcast.41), calls=%async_computation.1 | async-start | bytes 4194304 | tf_op jit(solution)/shard_map/all_to_all | solution.py:188

commit v2 on v1

v2 whole, which is shorter than its diff:
```python
import jax
import jax.numpy as jnp
from jax import lax
from jax.experimental import pallas as pl
from jax.experimental.pallas import tpu as pltpu
from jax.sharding import PartitionSpec as P


D = 1024
HEAD_DIM = 64
TILE = 128
NB = 8
PAIR = 2 * HEAD_DIM

score_scale = 0.125
SCALE2 = score_scale * 1.4426950408889634
SEND_PAIRS = (1, 1, 1, 1, 1, 1, 1, 1)
GROUPS = (1, 1, 1, 1, 1, 1, 1, 1)
PARTS = 2
EARLY = 6
SPLIT = 4
SIDE = 128


def pack_kernel(cols, keys_ref, values_ref, *outs):
    tok = keys_ref.shape[0]
    for (col, width), out in zip(cols, outs):
        out[:tok] = keys_ref[:, col : col + width]
        out[tok:] = values_ref[:, col : col + width]


def pack(keys, values, cols):
    tok, span = keys.shape[0], cols[-1][0] + cols[-1][1]
    return pl.pallas_call(
        lambda *refs: pack_kernel(cols, *refs),
        out_shape=[jax.ShapeDtypeStruct((2 * tok, width), keys.dtype) for _, width in cols],
        grid=(1,),
        in_specs=[pl.BlockSpec((tok, span), lambda i: (0, 0))] * 2,
        out_specs=[pl.BlockSpec((2 * tok, width), lambda i: (0, 0)) for _, width in cols],
        name="pack",
    )(keys, values)


def attend_kernel(sizes, *refs):
    pos_ref, live_ref, q_ref = refs[:3]
    blocks = refs[3 : 3 + 3 * len(sizes)]
    o_ref, kv, score_even, score_odd, peak_even, peak_odd, sems = refs[3 + 3 * len(sizes) :]
    tiles = q_ref.shape[0] // TILE
    pairs = q_ref.shape[1] // PAIR
    nb = pos_ref.shape[1]
    copies, col = [], 0
    for i, size in enumerate(sizes):
        for j in range(3):
            target = kv.at[pl.ds(2 * tiles * j, 2 * tiles), :, pl.ds(col, size * PAIR)]
            copies.append(pltpu.make_async_copy(blocks[3 * i + j], target, sems.at[3 * i + j]))
        col += size * PAIR
    for copy in copies:
        copy.start()
    for copy in copies:
        copy.wait()
    first = lax.broadcasted_iota(jnp.int32, (TILE, PAIR), 1) < HEAD_DIM
    ones = jnp.ones((16, 2 * TILE), jnp.bfloat16)
    count = tiles * pairs

    def place(index):
        t = index // pairs
        p = index - t * pairs
        return (
            t,
            pl.ds(pl.multiple_of(t * TILE, TILE), TILE),
            pl.ds(pl.multiple_of(p * PAIR, PAIR), PAIR),
        )

    def bias(t, j):
        return jnp.where(live_ref[t, j] > 0, jnp.float32(0.0), jnp.float32(-jnp.inf))

    def score(index, score_ref, peak_ref):
        t, rows, cols = place(index)
        q = q_ref[rows, cols]
        zero = jnp.zeros_like(q)
        two_heads = jnp.concatenate(
            [jnp.where(first, q, zero), jnp.where(first, zero, q)], axis=0
        )
        peak = None
        for j in range(nb):
            part = lax.dot_general(
                kv[pos_ref[t, j], :, cols],
                two_heads,
                (((1,), (1,)), ((), ())),
                preferred_element_type=jnp.float32,
            )
            score_ref[pl.ds(j * TILE, TILE), :] = part
            top = jnp.max(part.reshape(TILE // 8, 8, 2 * TILE), axis=0) + bias(t, j)
            peak = top if peak is None else jnp.maximum(peak, top)
        peak_ref[...] = peak

    def mix(index, score_ref, peak_ref):
        t, rows, cols = place(index)
        base = jnp.max(peak_ref[...], axis=0, keepdims=True) * SCALE2
        out = None
        for j in range(0, nb, 2):
            powers = [
                jnp.exp2(
                    score_ref[pl.ds(i * TILE, TILE), :] * SCALE2 - (base - bias(t, i))
                ).astype(jnp.bfloat16)
                for i in (j, j + 1)
            ]
            value = jnp.concatenate(
                [kv[pos_ref[t, i] + tiles, :, cols] for i in (j, j + 1)], axis=0
            )
            part = jnp.dot(
                jnp.concatenate([value.T, ones], axis=0),
                jnp.concatenate(powers, axis=0),
                preferred_element_type=jnp.float32,
            )
            out = part if out is None else out + part
        inverse = 1.0 / out[PAIR : PAIR + 1]
        both = jnp.concatenate(
            [
                out[:HEAD_DIM, :TILE] * inverse[:, :TILE],
                out[HEAD_DIM:PAIR, TILE:] * inverse[:, TILE:],
            ],
            axis=0,
        )
        o_ref[rows, cols] = both.T.astype(jnp.bfloat16)

    score(0, score_even, peak_even)

    def step(i, carry):
        score(2 * i + 1, score_odd, peak_odd)
        mix(2 * i, score_even, peak_even)
        score(jnp.minimum(2 * i + 2, count - 1), score_even, peak_even)
        mix(2 * i + 1, score_odd, peak_odd)
        return carry

    lax.fori_loop(0, count // 2, step, 0)


def attend(queries, col, sizes, blocks, position, live_bits):
    tok, width = queries.shape[0], sum(sizes) * PAIR
    if col % width:
        queries, col = lax.slice_in_dim(queries, col, col + width, axis=1), 0
    column = col // width
    tiles, nb = tok // TILE, position.shape[1]
    blocks = [block.reshape(2 * tiles, TILE, block.shape[1]) for block in blocks]
    return pl.pallas_call(
        lambda *refs: attend_kernel(sizes, *refs),
        out_shape=jax.ShapeDtypeStruct((tok, width), jnp.bfloat16),
        grid_spec=pltpu.PrefetchScalarGridSpec(
            num_scalar_prefetch=2,
            grid=(1,),
            in_specs=[pl.BlockSpec((tok, width), lambda i, *_: (0, column))]
            + [pl.BlockSpec(memory_space=pl.ANY)] * len(blocks),
            out_specs=pl.BlockSpec((tok, width), lambda i, *_: (0, 0)),
            scratch_shapes=[
                pltpu.VMEM((6 * tiles, TILE, width), jnp.bfloat16),
                pltpu.VMEM((nb * TILE, 2 * TILE), jnp.float32),
                pltpu.VMEM((nb * TILE, 2 * TILE), jnp.float32),
                pltpu.VMEM((8, 2 * TILE), jnp.float32),
                pltpu.VMEM((8, 2 * TILE), jnp.float32),
                pltpu.SemaphoreType.DMA((len(blocks),)),
            ],
        ),
        compiler_params=pltpu.CompilerParams(vmem_limit_bytes=24 << 20),
        cost_estimate=pl.CostEstimate(
            flops=4 * tok * NB * TILE * width * 2,
            transcendentals=tok * NB * TILE * width // HEAD_DIM,
            bytes_accessed=8 * tok * width * 2,
        ),
        name="attend",
    )(position, live_bits, queries, *blocks)


def norm_kernel(pre_ref, *refs):
    attn_refs, refs = refs[:-9], refs[-9:]
    w_ref, gain_ref, cell_ref, hidden_ref, normed_ref, out_ref, kept, staged, sems = refs
    attn = jnp.concatenate([ref[...] for ref in attn_refs], axis=1)
    hidden = pre_ref[...] + jnp.dot(attn, w_ref[...], preferred_element_type=jnp.float32)
    kept[...] = hidden
    copies = [pltpu.make_async_copy(kept, hidden_ref, sems.at[SPLIT])]
    copies[0].start()
    spread = jnp.mean(hidden * hidden, axis=-1, keepdims=True)
    normed = (hidden * lax.rsqrt(spread + 1e-06) * gain_ref[...]).astype(jnp.bfloat16)
    normed_ref[...] = normed
    step = staged.shape[0] // SPLIT
    for i in range(SPLIT):
        cells = lax.broadcasted_iota(jnp.int32, (step, cell_ref.shape[1]), 0) + i * step
        one_hot = (cells == cell_ref[...]).astype(jnp.bfloat16)
        staged[pl.ds(i * step, step)] = jnp.dot(
            one_hot, normed, preferred_element_type=jnp.float32
        ).astype(jnp.bfloat16)
        rows = pl.ds(i * step, step)
        copies.append(pltpu.make_async_copy(staged.at[rows], out_ref.at[rows], sems.at[i]))
        copies[-1].start()
    for copy in copies:
        copy.wait()


def norm_and_send(pre, attn, weights, depth, gain, cell, cells):
    tok, width = pre.shape
    rest = weights.shape[0] - depth
    if depth % rest:
        weights, depth = weights[depth:], 0
    whole = pl.BlockSpec(memory_space=pltpu.VMEM)
    return pl.pallas_call(
        norm_kernel,
        out_shape=[
            pltpu.HBM((tok, width), jnp.float32),
            jax.ShapeDtypeStruct((tok, width), jnp.bfloat16),
            pltpu.HBM((cells, width), jnp.bfloat16),
        ],
        grid=(1,),
        in_specs=[whole] * (1 + len(attn))
        + [pl.BlockSpec((rest, width), lambda i: (depth // rest, 0)), whole, whole],
        out_specs=[
            pl.BlockSpec(memory_space=pltpu.HBM),
            whole,
            pl.BlockSpec(memory_space=pltpu.HBM),
        ],
        scratch_shapes=[
            pltpu.VMEM((tok, width), jnp.float32),
            pltpu.VMEM((cells, width), jnp.bfloat16),
            pltpu.SemaphoreType.DMA((SPLIT + 1,)),
        ],
        compiler_params=pltpu.CompilerParams(vmem_limit_bytes=24 << 20),
        name="norm",
    )(pre, *attn, weights, gain[None, :], cell[None, :])


def chosen_rows(cell, back):
    cells = lax.broadcasted_iota(jnp.int32, (cell.shape[0], back.shape[0]), 1)
    one_hot = (cells == cell).astype(jnp.bfloat16)
    return jnp.dot(one_hot, back, preferred_element_type=jnp.float32)


def rows_kernel(hidden_ref, gate_ref, cell_ref, next_ref, back_ref, out_ref):
    width = hidden_ref.shape[1]
    rows = chosen_rows(cell_ref[...], back_ref[...])
    out_ref[:, :width] = hidden_ref[...] + gate_ref[...] * rows
    lane = lax.broadcasted_iota(jnp.int32, (out_ref.shape[0], SIDE), 1)
    out_ref[:, width:] = jnp.where(
        lane == 0, gate_ref[...], next_ref[...].astype(jnp.float32)
    )


def first_rows(hidden, gate, cell, next_cell, back):
    tok, width = hidden.shape
    return pl.pallas_call(
        rows_kernel,
        out_shape=jax.ShapeDtypeStruct((tok, width + SIDE), jnp.float32),
        compiler_params=pltpu.CompilerParams(vmem_limit_bytes=24 << 20),
        name="rows",
    )(hidden, gate, cell[:, None], next_cell[:, None], back)


def final_kernel(base_ref, back, out_ref, staged, sems):
    tok, width = staged.shape
    step = tok // SPLIT
    copies = []
    for i in range(SPLIT):
        rows = pl.ds(i * step, step)
        gate = base_ref[rows, width : width + 1]
        cell = base_ref[rows, width + 1 : width + 2].astype(jnp.int32)
        chosen = chosen_rows(cell, back[...])
        staged[rows] = (base_ref[rows, :width] + gate * chosen).astype(jnp.bfloat16)
        copies.append(pltpu.make_async_copy(staged.at[rows], out_ref.at[rows], sems.at[i]))
        copies[-1].start()
    for copy in copies:
        copy.wait()


def last_rows(base, back):
    shape = (base.shape[0], base.shape[1] - SIDE)
    return pl.pallas_call(
        final_kernel,
        out_shape=pltpu.HBM(shape, jnp.bfloat16),
        in_specs=[pl.BlockSpec(memory_space=pltpu.VMEM)] * 2,
        out_specs=pl.BlockSpec(memory_space=pltpu.HBM),
        scratch_shapes=[
            pltpu.VMEM(shape, jnp.bfloat16),
            pltpu.SemaphoreType.DMA((SPLIT,)),
        ],
        compiler_params=pltpu.CompilerParams(vmem_limit_bytes=16 << 20),
        name="final",
    )(base, back)


def expert_kernel(x_ref, up_ref, down_ref, o_ref, total):
    i = pl.program_id(0)
    last = pl.num_programs(0) - 1
    half = up_ref.shape[1] // 2
    part = None
    for s in range(2):
        lifted = jnp.dot(
            x_ref[...], up_ref[:, s * half : (s + 1) * half], preferred_element_type=jnp.float32
        )
        lifted = jax.nn.gelu(lifted, approximate=True).astype(jnp.bfloat16)
        down = jnp.dot(
            lifted, down_ref[s * half : (s + 1) * half, :], preferred_element_type=jnp.float32
        )
        part = down if part is None else part + down

    @pl.when(i == 0)
    def _():
        total[...] = part

    @pl.when(jnp.logical_and(i > 0, i < last))
    def _():
        total[...] += part

    @pl.when(i == last)
    def _():
        o_ref[...] = (total[...] + part).astype(jnp.bfloat16)


def run_expert(rows, up_matrix, down_matrix):
    count, hidden = rows.shape[0], up_matrix.shape[1]
    step = 1024
    return pl.pallas_call(
        expert_kernel,
        out_shape=jax.ShapeDtypeStruct((count, D), jnp.bfloat16),
        grid=(hidden // step,),
        in_specs=[
            pl.BlockSpec((count, D), lambda i: (0, 0)),
            pl.BlockSpec((D, step), lambda i: (0, i)),
            pl.BlockSpec((step, D), lambda i: (i, 0)),
        ],
        out_specs=pl.BlockSpec((count, D), lambda i: (0, 0)),
        scratch_shapes=[pltpu.VMEM((count, D), jnp.float32)],
        compiler_params=pltpu.CompilerParams(vmem_limit_bytes=58 << 20),
        cost_estimate=pl.CostEstimate(
            flops=4 * count * D * hidden, transcendentals=count * hidden, bytes_accessed=4 * D * hidden
        ),
        name="expert",
    )(rows, up_matrix, down_matrix)


def layer(
    tokens,
    queries,
    keys,
    values,
    neighbours,
    live_bits,
    out_proj,
    norm_gain,
    router,
    expert,
    slot,
    w_up,
    w_down,
):
    tok_dev = tokens.shape[0]
    tiles_dev = tok_dev // TILE
    experts = router.shape[1]
    cap = 2 * tok_dev // experts
    my_node = lax.axis_index("node")
    node_count = lax.axis_size("node")
    column_count = lax.axis_size("expert")
    swap = [(i, i ^ 1) for i in range(node_count)]
    onward = [(i, (i + 2 - 4 * (i % 2)) % node_count) for i in range(node_count)]
    is_odd = my_node % 2
    owner_node = neighbours // tiles_dev // column_count
    offset = (owner_node - my_node + node_count) % node_count
    near_offset = jnp.where(is_odd == 1, node_count - 1, 1)
    block_of = jnp.where(offset == 0, 0, jnp.where(offset == near_offset, 1, 2))
    position = block_of * (2 * tiles_dev) + neighbours % tiles_dev
    cols, col = [], 0
    for pairs in SEND_PAIRS:
        cols.append((col, pairs * PAIR))
        col += pairs * PAIR
    owns = pack(keys, values, cols[:1])
    owns += pack(keys, values, cols[1:])
    sent = []
    for i, own in enumerate(owns):
        near = lax.ppermute(own, "node", swap)
        far = lax.ppermute(near, "node", onward)
        sent.append((own, near, far))
    mixed, i, col = [], 0, 0
    for length in GROUPS:
        sizes = SEND_PAIRS[i : i + length]
        width = sum(sizes) * PAIR
        blocks = [block for chunk in sent[i : i + length] for block in chunk]
        mixed.append(attend(queries, col, sizes, blocks, position, live_bits))
        i, col = i + length, col + width
    part_cap = cap // PARTS
    slot_cell = expert * part_cap + slot % part_cap
    cells = [jnp.where(slot // part_cap == part, slot_cell, -1) for part in range(PARTS)]
    early = jnp.concatenate(mixed[:EARLY], axis=1)
    depth = early.shape[1]
    pre = tokens.astype(jnp.float32) + jnp.dot(
        early, out_proj[:depth], preferred_element_type=jnp.float32
    )
    hidden, normed, outgoing = norm_and_send(
        pre, mixed[EARLY:], out_proj, depth, norm_gain, cells[0], experts * part_cap
    )
    logits = jnp.dot(normed, router, preferred_element_type=jnp.float32)
    columns = lax.iota(jnp.int32, experts)
    chosen = jnp.sum(jnp.where(columns[None, :] == expert[:, None], logits, 0.0), axis=-1)
    gate = jax.nn.sigmoid(chosen)[:, None]
    layer_out = hidden
    for part in range(PARTS):
        if part:
            one_hot = lax.iota(jnp.int32, experts * part_cap)[:, None] == cells[part][None, :]
            outgoing = jnp.dot(
                one_hot.astype(jnp.bfloat16), normed, preferred_element_type=jnp.float32
            ).astype(jnp.bfloat16)
        block = lax.all_to_all(
            outgoing.reshape(experts, part_cap, D),
            ("node", "expert"),
            split_axis=0,
            concat_axis=0,
            tiled=True,
        )
        result = run_expert(block.reshape(-1, D), w_up[0], w_down[0])
        returned = lax.all_to_all(
            result.reshape(block.shape),
            ("node", "expert"),
            split_axis=0,
            concat_axis=0,
            tiled=True,
        )
        returned = returned.reshape(experts * part_cap, D)
        if part < PARTS - 1:
            layer_out = first_rows(layer_out, gate, cells[part], cells[part + 1], returned)
        else:
            layer_out = last_rows(layer_out, returned)
    return layer_out


def solution(mesh):
    in_specs = (
        P(("node", "expert"), None),
        P(("node", "expert"), None),
        P(("node", "expert"), None),
        P(("node", "expert"), None),
        P(("node", "expert"), None),
        P(("node", "expert"), None),
        P(),
        P(),
        P(),
        P(("node", "expert")),
        P(("node", "expert")),
        P(("node", "expert"), None, None),
        P(("node", "expert"), None, None),
    )
    out_specs = P(("node", "expert"), None)
    return jax.shard_map(layer, mesh=mesh, in_specs=in_specs, out_specs=out_specs, check_vma=False)
```

time: 221 us -> 207 us (0.937)
  blocking collectives: 53.4 us -> 0 us
  Pallas kernels: 27.3 us -> 61.1 us
  matrix products: 34.9 us -> 3.14 us
  starting transfers between devices: 17.2 us -> 42.4 us
  waiting for transfers between devices: 82.6 us -> 89.2 us
  local copies, waits for them, and re-layouts: 4.8 us -> 9.5 us
    all_to_all x1 -> x0, blocking collectives: 53.4 us -> none  [layer(): lax.all_to_all(outgoing.reshape(experts, 1, cap, D), ('node', 'expert'),...]
    all_to_all x0 -> x2, waiting for transfers between devices: none -> 35.9 us  [layer(): lax.all_to_all(outgoing.reshape(experts, part_cap, D), ('node', 'expert')...]
    pallas_call x4 -> x15, Pallas kernels: 27.3 us -> 61.1 us  [the longest x2 29.5 us: run_expert(): pl.pallas_call(expert_kernel, out_shape=jax.ShapeDtypeStruct((count, D),...]
    dot_general x4 -> x2, matrix products: 32.8 us -> 2.7 us  [the longest x1 1.69 us: layer(): jnp.dot(one_hot.astype(jnp.bfloat16), normed, preferred_element_type=jnp....]
    all_to_all x1 -> x2, waiting for transfers between devices: 46.6 us -> 27.9 us  [layer(): lax.all_to_all(result.reshape(block.shape), ('node', 'expert'), split_axi...]
    ppermute x4 -> x8, waiting for transfers between devices: 36 us -> 18.6 us  [layer(): near = lax.ppermute(own, 'node', swap)]
    all_to_all x0 -> x2, starting transfers between devices: none -> 9.38 us  [layer(): lax.all_to_all(outgoing.reshape(experts, part_cap, D), ('node', 'expert')...]
    ppermute x4 -> x8, starting transfers between devices: 5.27 us -> 12.9 us  [layer(): near = lax.ppermute(own, 'node', swap)]
  transfers between devices with their start and end apart: 9 -> 20, of which waited for: 5 -> 13; matrix products, arithmetic and copies ran while one was open for 1% -> 2% of each run, Pallas kernels for 9% -> 26%
where the time goes in v2:
time: 207 us; the launch traced here: 206 us
  waiting for transfers between devices  89.2 us (43%)
  Pallas kernels  61.1 us (30%)
  starting transfers between devices  42.4 us (20%)
  local copies, waits for them, and re-layouts  9.5 us (5%)
  matrix products  3.14 us (2%)
    all_to_all x2, waiting for transfers between devices, layer(): lax.all_to_all(outgoing.reshape(experts, part_cap, D), ('node', 'expert')...  35.9 us
    pallas_call x2, Pallas kernels, run_expert(): pl.pallas_call(expert_kernel, out_shape=jax.ShapeDtypeStruct((count, D),...  29.5 us
    all_to_all x2, waiting for transfers between devices, layer(): lax.all_to_all(result.reshape(block.shape), ('node', 'expert'), split_axi...  27.9 us
    pallas_call x8, Pallas kernels, attend(): pl.pallas_call(lambda *refs: attend_kernel(sizes, *refs), out_shape=jax.S...  22.4 us
    ppermute x8, waiting for transfers between devices, layer(): near = lax.ppermute(own, 'node', swap)  18.6 us
    ppermute x8, starting transfers between devices, layer(): near = lax.ppermute(own, 'node', swap)  12.9 us
    ppermute x8, starting transfers between devices, layer(): far = lax.ppermute(near, 'node', onward)  12.7 us
    all_to_all x2, starting transfers between devices, layer(): lax.all_to_all(outgoing.reshape(experts, part_cap, D), ('node', 'expert')...  9.38 us
  transfers between devices with their start and end apart: 20, of which 13 were waited for; matrix products, arithmetic and copies ran while one was open for 2% of the time, Pallas kernels for 26%

profile of v2, /device:TPU:0, one launch (start us, length us, event | category | flops | bytes accessed | tf_op | source)
XLA Modules:
  0.0 206.0 jit_solution(7024384176598817181)
XLA Ops:
  1.8 3.0 %collective-permute-start = (bf16[1024,128]{1,0:T(8,128)(2,1)}, bf16[1024,128]{1,0:T(8,128)(2,1)S(1)}, u32[]{:S(2)}, u32[]{:S(2)}) collective-permute-start(bf16[1024,128]{1,0:T(8,128)(2,1)} %pack.2), channel_id=1, source_target_pairs={{0,4},{4,0},{8,12},{12,8},{16,20},{20,16},{24,28},{28,24},{1,5},{5... | collective-permute-start | bytes 786440 | tf_op jit(solution)/shard_map/ppermute | solution.py:376
  4.8 2.9 %pack.3 = (bf16[1024,128]{1,0:T(8,128)(2,1)}, bf16[1024,128]{1,0:T(8,128)(2,1)}, bf16[1024,128]{1,0:T(8,128)(2,1)}, bf16[1024,128]{1,0:T(8,128)(2,1)}, bf16[1024...) custom-call(bf16[512,1024]{1,0:T(8,128)(2,1)} %refs_0_.3, bf16[512,1024]{1,0:T(8,128)(2,1)} %refs_1_.12), custom_call_target="tpu_custom_call" | custom-call | tf_op jit(solution)/shard_map/pack/pallas_call | solution.py:34
  7.7 2.0 collective-permute-start.4
  14.2 3.7 %collective-permute-done.2 = bf16[1024,128]{1,0:T(8,128)(2,1)S(1)} collective-permute-done((bf16[1024,128]{1,0:T(8,128)(2,1)}, bf16[1024,128]{1,0:T(8,128)(2,1)S(1)}, u32[]{:S(2)}, u32[]{:S(2)}) %collective-permute-start.2) | collective-permute-done | bytes 262176 | tf_op jit(solution)/shard_map/ppermute | solution.py:376
  17.8 2.0 collective-permute-start.1
  19.9 3.6 %collective-permute-done.4 = bf16[1024,128]{1,0:T(8,128)(2,1)S(1)} collective-permute-done((bf16[1024,128]{1,0:T(8,128)(2,1)}, bf16[1024,128]{1,0:T(8,128)(2,1)S(1)}, u32[]{:S(2)}, u32[]{:S(2)}) %collective-permute-start.4) | collective-permute-done | bytes 262176 | tf_op jit(solution)/shard_map/ppermute | solution.py:376
  23.5 2.0 collective-permute-start.3
  25.5 3.6 %collective-permute-done.6 = bf16[1024,128]{1,0:T(8,128)(2,1)S(1)} collective-permute-done((bf16[1024,128]{1,0:T(8,128)(2,1)}, bf16[1024,128]{1,0:T(8,128)(2,1)S(1)}, u32[]{:S(2)}, u32[]{:S(2)}) %collective-permute-start.6) | collective-permute-done | bytes 262176 | tf_op jit(solution)/shard_map/ppermute | solution.py:376
  31.0 3.7 %collective-permute-done.8 = bf16[1024,128]{1,0:T(8,128)(2,1)S(1)} collective-permute-done((bf16[1024,128]{1,0:T(8,128)(2,1)}, bf16[1024,128]{1,0:T(8,128)(2,1)S(1)}, u32[]{:S(2)}, u32[]{:S(2)}) %collective-permute-start.8) | collective-permute-done | bytes 262176 | tf_op jit(solution)/shard_map/ppermute | solution.py:376
  36.7 3.7 %collective-permute-done.10 = bf16[1024,128]{1,0:T(8,128)(2,1)S(1)} collective-permute-done((bf16[1024,128]{1,0:T(8,128)(2,1)}, bf16[1024,128]{1,0:T(8,128)(2,1)S(1)}, u32[]{:S(2)}, u32[]{:S(2)}) %collective-permute-start.10) | collective-permute-done | bytes 262176 | tf_op jit(solution)/shard_map/ppermute | solution.py:376
  40.3 2.0 collective-permute-start.5
  45.6 2.7 %attend.8 = bf16[512,128]{1,0:T(8,128)(2,1)S(1)} custom-call(s32[4,8]{1,0:T(4,128)S(1)} %fusion.7.refs_0_, s32[4,8]{1,0:T(4,128)S(1)} %copy-done.18, bf16[512,1024]{1,0:T(8,128)(2,1)S(1)} %copy-done.10, bf16[8,128,128]{2,1,0:T(8,128)(2,1)S(1)} %bitcast.45, bf16[8,128,128]{2,1,0:T(8,128)(2,1)S(1)} %bitcast.60, bf16[8,128,128]{2,1,0:T(8,128)(2,1)S(1)} %bitcast.64), custom_call_target="tpu_custom_call" | custom-call | flops 536870912 | bytes 1048576 | tf_op jit(solution)/shard_map/attend/pallas_call | solution.py:146
  49.3 3.6 %attend.9 = bf16[512,128]{1,0:T(8,128)(2,1)S(1)} custom-call(s32[4,8]{1,0:T(4,128)S(1)} %fusion.7.refs_0_, s32[4,8]{1,0:T(4,128)S(1)} %copy-done.18, bf16[512,1024]{1,0:T(8,128)(2,1)S(1)} %copy-done.10, bf16[8,128,128]{2,1,0:T(8,128)(2,1)S(1)} %bitcast.59, bf16[8,128,128]{2,1,0:T(8,128)(2,1)S(1)} %bitcast.61, bf16[8,128,128]{2,1,0:T(8,128)(2,1)} %bitcast.5.refs_5_), custom_call_target="tpu_custom_call" | custom-call | flops 536870912 | bytes 1048576 | tf_op jit(solution)/shard_map/attend/pallas_call | solution.py:146
  56.4 2.7 %attend.10 = bf16[512,128]{1,0:T(8,128)(2,1)S(1)} custom-call(s32[4,8]{1,0:T(4,128)S(1)} %fusion.7.refs_0_, s32[4,8]{1,0:T(4,128)S(1)} %copy-done.18, bf16[512,1024]{1,0:T(8,128)(2,1)S(1)} %copy-done.10, bf16[8,128,128]{2,1,0:T(8,128)(2,1)S(1)} %bitcast.54, bf16[8,128,128]{2,1,0:T(8,128)(2,1)S(1)} %bitcast.58, bf16[8,128,128]{2,1,0:T(8,128)(2,1)S(1)} %bitcast.66), custom_call_target="tpu_custom_call" | custom-call | flops 536870912 | bytes 1048576 | tf_op jit(solution)/shard_map/attend/pallas_call | solution.py:146
  59.1 2.7 %attend.11 = bf16[512,128]{1,0:T(8,128)(2,1)S(1)} custom-call(s32[4,8]{1,0:T(4,128)S(1)} %fusion.7.refs_0_, s32[4,8]{1,0:T(4,128)S(1)} %copy-done.18, bf16[512,1024]{1,0:T(8,128)(2,1)S(1)} %copy-done.10, bf16[8,128,128]{2,1,0:T(8,128)(2,1)S(1)} %bitcast.53, bf16[8,128,128]{2,1,0:T(8,128)(2,1)S(1)} %bitcast.57, bf16[8,128,128]{2,1,0:T(8,128)(2,1)S(1)} %bitcast.67), custom_call_target="tpu_custom_call" | custom-call | flops 536870912 | bytes 1048576 | tf_op jit(solution)/shard_map/attend/pallas_call | solution.py:146
  62.8 2.7 %attend.12 = bf16[512,128]{1,0:T(8,128)(2,1)S(1)} custom-call(s32[4,8]{1,0:T(4,128)S(1)} %fusion.7.refs_0_, s32[4,8]{1,0:T(4,128)S(1)} %copy-done.18, bf16[512,1024]{1,0:T(8,128)(2,1)S(1)} %copy-done.10, bf16[8,128,128]{2,1,0:T(8,128)(2,1)S(1)} %bitcast.52, bf16[8,128,128]{2,1,0:T(8,128)(2,1)S(1)} %bitcast.56, bf16[8,128,128]{2,1,0:T(8,128)(2,1)S(1)} %bitcast.68), custom_call_target="tpu_custom_call" | custom-call | flops 536870912 | bytes 1048576 | tf_op jit(solution)/shard_map/attend/pallas_call | solution.py:146
  65.5 2.8 %collective-permute-done.11 = bf16[1024,128]{1,0:T(8,128)(2,1)S(1)} collective-permute-done((bf16[1024,128]{1,0:T(8,128)(2,1)S(1)}, bf16[1024,128]{1,0:T(8,128)(2,1)S(1)}, u32[]{:S(2)}, u32[]{:S(2)}) %collective-permute-start.11) | collective-permute-done | bytes 262176 | tf_op jit(solution)/shard_map/ppermute | solution.py:377
  68.4 2.7 %attend.13 = bf16[512,128]{1,0:T(8,128)(2,1)S(1)} custom-call(s32[4,8]{1,0:T(4,128)S(1)} %fusion.7.refs_0_, s32[4,8]{1,0:T(4,128)S(1)} %copy-done.18, bf16[512,1024]{1,0:T(8,128)(2,1)S(1)} %copy-done.10, bf16[8,128,128]{2,1,0:T(8,128)(2,1)S(1)} %bitcast.51, bf16[8,128,128]{2,1,0:T(8,128)(2,1)S(1)} %bitcast.55, bf16[8,128,128]{2,1,0:T(8,128)(2,1)S(1)} %bitcast.70), custom_call_target="tpu_custom_call" | custom-call | flops 536870912 | bytes 1048576 | tf_op jit(solution)/shard_map/attend/pallas_call | solution.py:146
  71.2 2.8 %collective-permute-done.13 = bf16[1024,128]{1,0:T(8,128)(2,1)S(1)} collective-permute-done((bf16[1024,128]{1,0:T(8,128)(2,1)S(1)}, bf16[1024,128]{1,0:T(8,128)(2,1)S(1)}, u32[]{:S(2)}, u32[]{:S(2)}) %collective-permute-start.13) | collective-permute-done | bytes 262176 | tf_op jit(solution)/shard_map/ppermute | solution.py:377
  74.0 2.7 %attend.14.refs_0_ = bf16[512,128]{1,0:T(8,128)(2,1)S(1)} custom-call(s32[4,8]{1,0:T(4,128)S(1)} %fusion.7.refs_0_, s32[4,8]{1,0:T(4,128)S(1)} %copy-done.18, bf16[512,1024]{1,0:T(8,128)(2,1)S(1)} %copy-done.10, bf16[8,128,128]{2,1,0:T(8,128)(2,1)S(1)} %bitcast.50, bf16[8,128,128]{2,1,0:T(8,128)(2,1)S(1)} %bitcast.63, bf16[8,128,128]{2,1,0:T(8,128)(2,1)S(1)} %bitcast.69), custom_call_target="tpu_custom_call" | custom-call | flops 536870912 | bytes 1048576 | tf_op jit(solution)/shard_map/attend/pallas_call | solution.py:146
  76.8 2.7 %attend.15.refs_1_ = bf16[512,128]{1,0:T(8,128)(2,1)S(1)} custom-call(s32[4,8]{1,0:T(4,128)S(1)} %fusion.7.refs_0_, s32[4,8]{1,0:T(4,128)S(1)} %copy-done.18, bf16[512,1024]{1,0:T(8,128)(2,1)S(1)} %copy-done.10, bf16[8,128,128]{2,1,0:T(8,128)(2,1)S(1)} %bitcast.49, bf16[8,128,128]{2,1,0:T(8,128)(2,1)S(1)} %bitcast.62, bf16[8,128,128]{2,1,0:T(8,128)(2,1)S(1)} %bitcast.65), custom_call_target="tpu_custom_call" | custom-call | flops 536870912 | bytes 1048576 | tf_op jit(solution)/shard_map/attend/pallas_call | solution.py:146
  80.6 2.2 %norm.1 = (f32[512,1024]{1,0:T(8,128)}, bf16[512,1024]{1,0:T(8,128)(2,1)S(1)}, bf16[512,1024]{1,0:T(8,128)(2,1)}) custom-call(f32[512,1024]{1,0:T(8,128)S(1)} %convert_add_fusion.pre_ref, bf16[512,128]{1,0:T(8,128)(2,1)S(1)} %attend.14.refs_0_, bf16[512,128]{1,0:T(8,128)(2,1)S(1)} %attend.15.refs_1_, bf16[1024,1024]{1,0:T(8,128)(2,1)S(1)} %copy-done.4, ...), custom_call_target="tpu_custom_call" | custom-call | tf_op jit(solution)/shard_map/norm/pallas_call | solution.py:205
  82.8 5.8 %all-to-all-start = ((bf16[32,16,1024]{2,1,0:T(8,128)(2,1)}), bf16[32,16,1024]{2,1,0:T(8,128)(2,1)S(1)}, u32[]{:S(2)}, u32[]{:S(2)}) async-start(bf16[32,16,1024]{2,1,0:T(8,128)(2,1)} %bitcast.74), calls=%async_computation | async-start | bytes 2097152 | tf_op jit(solution)/shard_map/all_to_all | solution.py:408
  90.2 24.5 %all-to-all-done = bf16[32,16,1024]{2,1,0:T(8,128)(2,1)S(1)} async-done(((bf16[32,16,1024]{2,1,0:T(8,128)(2,1)}), bf16[32,16,1024]{2,1,0:T(8,128)(2,1)S(1)}, u32[]{:S(2)}, u32[]{:S(2)}) %all-to-all-start) | async-done | bytes 1048608 | tf_op jit(solution)/shard_map/all_to_all | solution.py:408
  114.7 3.6 %all-to-all-start.2 = ((bf16[32,16,1024]{2,1,0:T(8,128)(2,1)}), bf16[32,16,1024]{2,1,0:T(8,128)(2,1)S(1)}, u32[]{:S(2)}, u32[]{:S(2)}) async-start(bf16[32,16,1024]{2,1,0:T(8,128)(2,1)} %bitcast.76), calls=%async_computation.2 | async-start | bytes 2097152 | tf_op jit(solution)/shard_map/all_to_all | solution.py:408
  118.4 14.8 %expert.2 = bf16[512,1024]{1,0:T(8,128)(2,1)} custom-call(bf16[512,1024]{1,0:T(8,128)(2,1)} %bitcast.72, bf16[1024,4096]{1,0:T(8,128)(2,1)} %bitcast.79, bf16[4096,1024]{1,0:T(8,128)(2,1)} %bitcast.81), custom_call_target="tpu_custom_call" | custom-call | flops 8589934592 | bytes 16777216 | tf_op jit(solution)/shard_map/expert/pallas_call | solution.py:319
  133.2 11.4 %all-to-all-done.2 = bf16[32,16,1024]{2,1,0:T(8,128)(2,1)S(1)} async-done(((bf16[32,16,1024]{2,1,0:T(8,128)(2,1)}), bf16[32,16,1024]{2,1,0:T(8,128)(2,1)S(1)}, u32[]{:S(2)}, u32[]{:S(2)}) %all-to-all-start.2) | async-done | bytes 1048608 | tf_op jit(solution)/shard_map/all_to_all | solution.py:408
  144.6 3.8 %all-to-all-start.1 = ((bf16[32,16,1024]{2,1,0:T(8,128)(2,1)}), bf16[32,16,1024]{2,1,0:T(8,128)(2,1)S(1)}, u32[]{:S(2)}, u32[]{:S(2)}) async-start(bf16[32,16,1024]{2,1,0:T(8,128)(2,1)} %bitcast.75), calls=%async_computation.1 | async-start | bytes 2097152 | tf_op jit(solution)/shard_map/all_to_all | solution.py:416
  148.4 14.8 %expert.3 = bf16[512,1024]{1,0:T(8,128)(2,1)} custom-call(bf16[512,1024]{1,0:T(8,128)(2,1)} %bitcast.73, bf16[1024,4096]{1,0:T(8,128)(2,1)} %bitcast.80, bf16[4096,1024]{1,0:T(8,128)(2,1)} %bitcast.82), custom_call_target="tpu_custom_call" | custom-call | flops 8589934592 | bytes 16777216 | tf_op jit(solution)/shard_map/expert/pallas_call | solution.py:319
  163.2 11.2 %all-to-all-done.1 = bf16[32,16,1024]{2,1,0:T(8,128)(2,1)S(1)} async-done(((bf16[32,16,1024]{2,1,0:T(8,128)(2,1)}), bf16[32,16,1024]{2,1,0:T(8,128)(2,1)S(1)}, u32[]{:S(2)}, u32[]{:S(2)}) %all-to-all-start.1) | async-done | bytes 1048608 | tf_op jit(solution)/shard_map/all_to_all | solution.py:416
  174.4 3.6 %all-to-all-start.3 = ((bf16[32,16,1024]{2,1,0:T(8,128)(2,1)}), bf16[32,16,1024]{2,1,0:T(8,128)(2,1)S(1)}, u32[]{:S(2)}, u32[]{:S(2)}) async-start(bf16[32,16,1024]{2,1,0:T(8,128)(2,1)} %bitcast.71), calls=%async_computation.3 | async-start | bytes 2097152 | tf_op jit(solution)/shard_map/all_to_all | solution.py:416
  187.5 16.7 %all-to-all-done.3 = bf16[32,16,1024]{2,1,0:T(8,128)(2,1)S(1)} async-done(((bf16[32,16,1024]{2,1,0:T(8,128)(2,1)}), bf16[32,16,1024]{2,1,0:T(8,128)(2,1)S(1)}, u32[]{:S(2)}, u32[]{:S(2)}) %all-to-all-start.3) | async-done | bytes 1048608 | tf_op jit(solution)/shard_map/all_to_all | solution.py:416
  (88 shorter events, 32.8 us)
Async XLA Ops:
  0.0 179.8 %copy-start = (bf16[1024,32]{0,1:T(8,128)(2,1)S(1)}, bf16[1024,32]{0,1:T(8,128)(2,1)}, u32[]{:S(2)}) copy-start(bf16[1024,32]{0,1:T(8,128)(2,1)} %param.21) | copy-start | bytes 196612
  0.0 25.5 %copy-start.21 = (s32[512]{0:T(512)S(1)}, s32[512]{0:T(512)}, u32[]{:S(2)}) copy-start(s32[512]{0:T(512)} %param.22) | copy-start | bytes 6148
  0.0 25.5 %copy-start.23 = (s32[512]{0:T(512)S(1)}, s32[512]{0:T(512)}, u32[]{:S(2)}) copy-start(s32[512]{0:T(512)} %param.23) | copy-start | bytes 6148
  0.0 45.5 %copy-start.22 = (s32[4,8]{1,0:T(4,128)S(1)}, s32[4,8]{1,0:T(4,128)}, u32[]{:S(2)}) copy-start(s32[4,8]{1,0:T(4,128)} %param.17) | copy-start | bytes 388
  0.0 45.5 %copy-start.18 = (s32[4,8]{1,0:T(4,128)S(1)}, s32[4,8]{1,0:T(4,128)}, u32[]{:S(2)}) copy-start(s32[4,8]{1,0:T(4,128)} %refs_1_.19) | copy-start | bytes 388
  0.0 45.5 %copy-start.10 = (bf16[512,1024]{1,0:T(8,128)(2,1)S(1)}, bf16[512,1024]{1,0:T(8,128)(2,1)}, u32[]{:S(2)}) copy-start(bf16[512,1024]{1,0:T(8,128)(2,1)} %refs_2_.16) | copy-start | bytes 3145732
  1.8 43.8 %copy-start.8 = (bf16[1024,128]{1,0:T(8,128)(2,1)S(1)}, bf16[1024,128]{1,0:T(8,128)(2,1)}, u32[]{:S(2)}) copy-start(bf16[1024,128]{1,0:T(8,128)(2,1)} %pack.2) | copy-start | bytes 786436
  1.8 10.4 %collective-permute-start = (bf16[1024,128]{1,0:T(8,128)(2,1)}, bf16[1024,128]{1,0:T(8,128)(2,1)S(1)}, u32[]{:S(2)}, u32[]{:S(2)}) collective-permute-start(bf16[1024,128]{1,0:T(8,128)(2,1)} %pack.2), channel_id=1, source_target_pairs={{0,4},{4,0},{8,12},{12,8},{16,20},{20,16},{24,28},{28,24},{1,5},{5... | collective-permute-start | bytes 786440 | tf_op jit(solution)/shard_map/ppermute | solution.py:376
  7.7 48.7 %copy-start.16 = (bf16[1024,128]{1,0:T(8,128)(2,1)S(1)}, bf16[1024,128]{1,0:T(8,128)(2,1)}, u32[]{:S(2)}) copy-start(bf16[1024,128]{1,0:T(8,128)(2,1)} %get-tuple-element.16) | copy-start | bytes 786436
  7.7 10.2 %collective-permute-start.2 = (bf16[1024,128]{1,0:T(8,128)(2,1)}, bf16[1024,128]{1,0:T(8,128)(2,1)S(1)}, u32[]{:S(2)}, u32[]{:S(2)}) collective-permute-start(bf16[1024,128]{1,0:T(8,128)(2,1)} %get-tuple-element.15), channel_id=1, source_target_pairs={{0,4},{4,0},{8,12},{12,8},{16,20},{20,16},{24,28},{28,24},{1,5},{5... | collective-permute-start | bytes 786440 | tf_op jit(solution)/shard_map/ppermute | solution.py:376
  7.7 15.7 %collective-permute-start.4 = (bf16[1024,128]{1,0:T(8,128)(2,1)}, bf16[1024,128]{1,0:T(8,128)(2,1)S(1)}, u32[]{:S(2)}, u32[]{:S(2)}) collective-permute-start(bf16[1024,128]{1,0:T(8,128)(2,1)} %get-tuple-element.16), channel_id=1, source_target_pairs={{0,4},{4,0},{8,12},{12,8},{16,20},{20,16},{24,28},{28,24},{1,5},{5... | collective-permute-start | bytes 786440 | tf_op jit(solution)/shard_map/ppermute | solution.py:376
  9.7 19.4 %collective-permute-start.6 = (bf16[1024,128]{1,0:T(8,128)(2,1)}, bf16[1024,128]{1,0:T(8,128)(2,1)S(1)}, u32[]{:S(2)}, u32[]{:S(2)}) collective-permute-start(bf16[1024,128]{1,0:T(8,128)(2,1)} %get-tuple-element.17), channel_id=1, source_target_pairs={{0,4},{4,0},{8,12},{12,8},{16,20},{20,16},{24,28},{28,24},{1,5},{5... | collective-permute-start | bytes 786440 | tf_op jit(solution)/shard_map/ppermute | solution.py:376
  9.8 24.9 %collective-permute-start.8 = (bf16[1024,128]{1,0:T(8,128)(2,1)}, bf16[1024,128]{1,0:T(8,128)(2,1)S(1)}, u32[]{:S(2)}, u32[]{:S(2)}) collective-permute-start(bf16[1024,128]{1,0:T(8,128)(2,1)} %get-tuple-element.18), channel_id=1, source_target_pairs={{0,4},{4,0},{8,12},{12,8},{16,20},{20,16},{24,28},{28,24},{1,5},{5... | collective-permute-start | bytes 786440 | tf_op jit(solution)/shard_map/ppermute | solution.py:376
  12.2 28.1 %collective-permute-start.10 = (bf16[1024,128]{1,0:T(8,128)(2,1)}, bf16[1024,128]{1,0:T(8,128)(2,1)S(1)}, u32[]{:S(2)}, u32[]{:S(2)}) collective-permute-start(bf16[1024,128]{1,0:T(8,128)(2,1)} %get-tuple-element.19), channel_id=1, source_target_pairs={{0,4},{4,0},{8,12},{12,8},{16,20},{20,16},{24,28},{28,24},{1,5},{5... | collective-permute-start | bytes 786440 | tf_op jit(solution)/shard_map/ppermute | solution.py:376
  17.8 24.5 %collective-permute-start.1 = (bf16[1024,128]{1,0:T(8,128)(2,1)S(1)}, bf16[1024,128]{1,0:T(8,128)(2,1)S(1)}, u32[]{:S(2)}, u32[]{:S(2)}) collective-permute-start(bf16[1024,128]{1,0:T(8,128)(2,1)S(1)} %collective-permute-done), channel_id=1, source_target_pairs={{0,8},{4,28},{8,16},{12,4},{16,24},{20,12},{24,0},{28,20},{1,9},{5... | collective-permute-start | bytes 786440 | tf_op jit(solution)/shard_map/ppermute | solution.py:377
  23.5 20.5 %collective-permute-start.3 = (bf16[1024,128]{1,0:T(8,128)(2,1)S(1)}, bf16[1024,128]{1,0:T(8,128)(2,1)}, u32[]{:S(2)}, u32[]{:S(2)}) collective-permute-start(bf16[1024,128]{1,0:T(8,128)(2,1)S(1)} %collective-permute-done.2), channel_id=1, source_target_pairs={{0,8},{4,28},{8,16},{12,4},{16,24},{20,12},{24,0},{28,20},{1,9},{5... | collective-permute-start | bytes 786440 | tf_op jit(solution)/shard_map/ppermute | solution.py:377
  29.1 23.8 %collective-permute-start.12 = (bf16[1024,128]{1,0:T(8,128)(2,1)}, bf16[1024,128]{1,0:T(8,128)(2,1)S(1)}, u32[]{:S(2)}, u32[]{:S(2)}) collective-permute-start(bf16[1024,128]{1,0:T(8,128)(2,1)} %get-tuple-element.20), channel_id=1, source_target_pairs={{0,4},{4,0},{8,12},{12,8},{16,20},{20,16},{24,28},{28,24},{1,5},{5... | collective-permute-start | bytes 786440 | tf_op jit(solution)/shard_map/ppermute | solution.py:376
  34.7 18.3 %collective-permute-start.14 = (bf16[1024,128]{1,0:T(8,128)(2,1)}, bf16[1024,128]{1,0:T(8,128)(2,1)S(1)}, u32[]{:S(2)}, u32[]{:S(2)}) collective-permute-start(bf16[1024,128]{1,0:T(8,128)(2,1)} %get-tuple-element.21), channel_id=1, source_target_pairs={{0,4},{4,0},{8,12},{12,8},{16,20},{20,16},{24,28},{28,24},{1,5},{5... | collective-permute-start | bytes 786440 | tf_op jit(solution)/shard_map/ppermute | solution.py:376
  40.3 14.5 %collective-permute-start.5 = (bf16[1024,128]{1,0:T(8,128)(2,1)S(1)}, bf16[1024,128]{1,0:T(8,128)(2,1)S(1)}, u32[]{:S(2)}, u32[]{:S(2)}) collective-permute-start(bf16[1024,128]{1,0:T(8,128)(2,1)S(1)} %collective-permute-done.4), channel_id=1, source_target_pairs={{0,8},{4,28},{8,16},{12,4},{16,24},{20,12},{24,0},{28,20},{1,9},{5... | collective-permute-start | bytes 786440 | tf_op jit(solution)/shard_map/ppermute | solution.py:377
  42.4 16.7 %collective-permute-start.7 = (bf16[1024,128]{1,0:T(8,128)(2,1)S(1)}, bf16[1024,128]{1,0:T(8,128)(2,1)S(1)}, u32[]{:S(2)}, u32[]{:S(2)}) collective-permute-start(bf16[1024,128]{1,0:T(8,128)(2,1)S(1)} %collective-permute-done.6), channel_id=1, source_target_pairs={{0,8},{4,28},{8,16},{12,4},{16,24},{20,12},{24,0},{28,20},{1,9},{5... | collective-permute-start | bytes 786440 | tf_op jit(solution)/shard_map/ppermute | solution.py:377
  43.9 18.8 %collective-permute-start.9 = (bf16[1024,128]{1,0:T(8,128)(2,1)S(1)}, bf16[1024,128]{1,0:T(8,128)(2,1)S(1)}, u32[]{:S(2)}, u32[]{:S(2)}) collective-permute-start(bf16[1024,128]{1,0:T(8,128)(2,1)S(1)} %collective-permute-done.8), channel_id=1, source_target_pairs={{0,8},{4,28},{8,16},{12,4},{16,24},{20,12},{24,0},{28,20},{1,9},{5... | collective-permute-start | bytes 786440 | tf_op jit(solution)/shard_map/ppermute | solution.py:377
  48.3 10.8 %copy-start.15 = (bf16[1024,128]{1,0:T(8,128)(2,1)S(1)}, bf16[1024,128]{1,0:T(8,128)(2,1)}, u32[]{:S(2)}) copy-start(bf16[1024,128]{1,0:T(8,128)(2,1)} %get-tuple-element.17) | copy-start | bytes 786436
  52.9 9.9 %copy-start.14 = (bf16[1024,128]{1,0:T(8,128)(2,1)S(1)}, bf16[1024,128]{1,0:T(8,128)(2,1)}, u32[]{:S(2)}) copy-start(bf16[1024,128]{1,0:T(8,128)(2,1)} %get-tuple-element.18) | copy-start | bytes 786436
  52.9 15.5 %collective-permute-start.11 = (bf16[1024,128]{1,0:T(8,128)(2,1)S(1)}, bf16[1024,128]{1,0:T(8,128)(2,1)S(1)}, u32[]{:S(2)}, u32[]{:S(2)}) collective-permute-start(bf16[1024,128]{1,0:T(8,128)(2,1)S(1)} %collective-permute-done.10), channel_id=1, source_target_pairs={{0,8},{4,28},{8,16},{12,4},{16,24},{20,12},{24,0},{28,20},{1,9},{5... | collective-permute-start | bytes 786440 | tf_op jit(solution)/shard_map/ppermute | solution.py:377
  53.0 21.0 %collective-permute-start.13 = (bf16[1024,128]{1,0:T(8,128)(2,1)S(1)}, bf16[1024,128]{1,0:T(8,128)(2,1)S(1)}, u32[]{:S(2)}, u32[]{:S(2)}) collective-permute-start(bf16[1024,128]{1,0:T(8,128)(2,1)S(1)} %collective-permute-done.12), channel_id=1, source_target_pairs={{0,8},{4,28},{8,16},{12,4},{16,24},{20,12},{24,0},{28,20},{1,9},{5... | collective-permute-start | bytes 786440 | tf_op jit(solution)/shard_map/ppermute | solution.py:377
  54.8 22.1 %collective-permute-start.15 = (bf16[1024,128]{1,0:T(8,128)(2,1)S(1)}, bf16[1024,128]{1,0:T(8,128)(2,1)S(1)}, u32[]{:S(2)}, u32[]{:S(2)}) collective-permute-start(bf16[1024,128]{1,0:T(8,128)(2,1)S(1)} %collective-permute-done.14), channel_id=1, source_target_pairs={{0,8},{4,28},{8,16},{12,4},{16,24},{20,12},{24,0},{28,20},{1,9},{5... | collective-permute-start | bytes 786440 | tf_op jit(solution)/shard_map/ppermute | solution.py:377
  59.1 9.3 %copy-start.13 = (bf16[1024,128]{1,0:T(8,128)(2,1)S(1)}, bf16[1024,128]{1,0:T(8,128)(2,1)}, u32[]{:S(2)}) copy-start(bf16[1024,128]{1,0:T(8,128)(2,1)} %get-tuple-element.19) | copy-start | bytes 786436
  62.8 11.2 %copy-start.12 = (bf16[1024,128]{1,0:T(8,128)(2,1)S(1)}, bf16[1024,128]{1,0:T(8,128)(2,1)}, u32[]{:S(2)}) copy-start(bf16[1024,128]{1,0:T(8,128)(2,1)} %get-tuple-element.20) | copy-start | bytes 786436
  82.8 32.0 %all-to-all-start = ((bf16[32,16,1024]{2,1,0:T(8,128)(2,1)}), bf16[32,16,1024]{2,1,0:T(8,128)(2,1)S(1)}, u32[]{:S(2)}, u32[]{:S(2)}) async-start(bf16[32,16,1024]{2,1,0:T(8,128)(2,1)} %bitcast.74), calls=%async_computation | async-start | bytes 2097152 | tf_op jit(solution)/shard_map/all_to_all | solution.py:408
  114.7 29.8 %all-to-all-start.2 = ((bf16[32,16,1024]{2,1,0:T(8,128)(2,1)}), bf16[32,16,1024]{2,1,0:T(8,128)(2,1)S(1)}, u32[]{:S(2)}, u32[]{:S(2)}) async-start(bf16[32,16,1024]{2,1,0:T(8,128)(2,1)} %bitcast.76), calls=%async_computation.2 | async-start | bytes 2097152 | tf_op jit(solution)/shard_map/all_to_all | solution.py:408
  144.6 29.8 %all-to-all-start.1 = ((bf16[32,16,1024]{2,1,0:T(8,128)(2,1)}), bf16[32,16,1024]{2,1,0:T(8,128)(2,1)S(1)}, u32[]{:S(2)}, u32[]{:S(2)}) async-start(bf16[32,16,1024]{2,1,0:T(8,128)(2,1)} %bitcast.75), calls=%async_computation.1 | async-start | bytes 2097152 | tf_op jit(solution)/shard_map/all_to_all | solution.py:416
  174.4 29.8 %all-to-all-start.3 = ((bf16[32,16,1024]{2,1,0:T(8,128)(2,1)}), bf16[32,16,1024]{2,1,0:T(8,128)(2,1)S(1)}, u32[]{:S(2)}, u32[]{:S(2)}) async-start(bf16[32,16,1024]{2,1,0:T(8,128)(2,1)} %bitcast.71), calls=%async_computation.3 | async-start | bytes 2097152 | tf_op jit(solution)/shard_map/all_to_all | solution.py:416
  (13 other events, 41.3 us)

commit v3 on v2

--- a/solution.py
+++ b/solution.py
@@ -17,8 +17,9 @@
 SEND_PAIRS = (1, 1, 1, 1, 1, 1, 1, 1)
 GROUPS = (1, 1, 1, 1, 1, 1, 1, 1)
 PARTS = 2
-EARLY = 6
+EARLY = 7
 SPLIT = 4
+UNROLLED = 4
 SIDE = 128
 
 
@@ -65,6 +66,8 @@
     def place(index):
         t = index // pairs
         p = index - t * pairs
+        if isinstance(index, int):
+            return t, pl.ds(t * TILE, TILE), pl.ds(p * PAIR, PAIR)
         return (
             t,
             pl.ds(pl.multiple_of(t * TILE, TILE), TILE),
@@ -124,13 +127,20 @@
         )
         o_ref[rows, cols] = both.T.astype(jnp.bfloat16)
 
-    score(0, score_even, peak_even)
+    slots = ((score_even, peak_even), (score_odd, peak_odd))
+    score(0, *slots[0])
+    if count <= UNROLLED:
+        for index in range(count):
+            if index + 1 < count:
+                score(index + 1, *slots[(index + 1) % 2])
+            mix(index, *slots[index % 2])
+        return
 
     def step(i, carry):
-        score(2 * i + 1, score_odd, peak_odd)
-        mix(2 * i, score_even, peak_even)
-        score(jnp.minimum(2 * i + 2, count - 1), score_even, peak_even)
-        mix(2 * i + 1, score_odd, peak_odd)
+        for half in range(2):
+            index = 2 * i + half
+            score(jnp.minimum(index + 1, count - 1), *slots[1 - half])
+            mix(index, *slots[half])
         return carry
 
     lax.fori_loop(0, count // 2, step, 0)
@@ -174,14 +184,24 @@
 def norm_kernel(pre_ref, *refs):
     attn_refs, refs = refs[:-9], refs[-9:]
     w_ref, gain_ref, cell_ref, hidden_ref, normed_ref, out_ref, kept, staged, sems = refs
-    attn = jnp.concatenate([ref[...] for ref in attn_refs], axis=1)
-    hidden = pre_ref[...] + jnp.dot(attn, w_ref[...], preferred_element_type=jnp.float32)
-    kept[...] = hidden
-    copies = [pltpu.make_async_copy(kept, hidden_ref, sems.at[SPLIT])]
-    copies[0].start()
-    spread = jnp.mean(hidden * hidden, axis=-1, keepdims=True)
-    normed = (hidden * lax.rsqrt(spread + 1e-06) * gain_ref[...]).astype(jnp.bfloat16)
-    normed_ref[...] = normed
+    copies = []
+    step = pre_ref.shape[0] // SPLIT
+    for i in range(SPLIT):
+        rows = pl.ds(i * step, step)
+        attn = jnp.concatenate([ref[rows] for ref in attn_refs], axis=1)
+        hidden = pre_ref[rows] + jnp.dot(
+            attn, w_ref[...], preferred_element_type=jnp.float32
+        )
+        kept[rows] = hidden
+        copies.append(
+            pltpu.make_async_copy(kept.at[rows], hidden_ref.at[rows], sems.at[SPLIT + i])
+        )
+        copies[-1].start()
+        spread = jnp.mean(hidden * hidden, axis=-1, keepdims=True)
+        normed_ref[rows] = (hidden * lax.rsqrt(spread + 1e-06) * gain_ref[...]).astype(
+            jnp.bfloat16
+        )
+    normed = normed_ref[...]
     step = staged.shape[0] // SPLIT
     for i in range(SPLIT):
         cells = lax.broadcasted_iota(jnp.int32, (step, cell_ref.shape[1]), 0) + i * step
@@ -198,9 +218,7 @@
 
 def norm_and_send(pre, attn, weights, depth, gain, cell, cells):
     tok, width = pre.shape
-    rest = weights.shape[0] - depth
-    if depth % rest:
-        weights, depth = weights[depth:], 0
+    weights = weights[depth:]
     whole = pl.BlockSpec(memory_space=pltpu.VMEM)
     return pl.pallas_call(
         norm_kernel,
@@ -211,7 +229,7 @@
         ],
         grid=(1,),
         in_specs=[whole] * (1 + len(attn))
-        + [pl.BlockSpec((rest, width), lambda i: (depth // rest, 0)), whole, whole],
+        + [whole] * 3,
         out_specs=[
             pl.BlockSpec(memory_space=pltpu.HBM),
             whole,
@@ -220,7 +238,7 @@
         scratch_shapes=[
             pltpu.VMEM((tok, width), jnp.float32),
             pltpu.VMEM((cells, width), jnp.bfloat16),
-            pltpu.SemaphoreType.DMA((SPLIT + 1,)),
+            pltpu.SemaphoreType.DMA((2 * SPLIT,)),
         ],
         compiler_params=pltpu.CompilerParams(vmem_limit_bytes=24 << 20),
         name="norm",

time: 207 us -> 201 us (0.971)
  Pallas kernels: 61.1 us -> 56.6 us
    pallas_call x8, Pallas kernels: 22.4 us -> 17.9 us  [attend(): pl.pallas_call(lambda *refs: attend_kernel(sizes, *refs), out_shape=jax.S...]
    unnamed x55 -> x60, local copies, waits for them, and re-layouts: 6.88 us -> 6.64 us
  transfers between devices with their start and end apart: 20 -> 20, of which waited for: 13 -> 12; matrix products, arithmetic and copies ran while one was open for 2% -> 4% of each run, Pallas kernels for 26% -> 24%
where the time goes in v3:
time: 201 us; the launch traced here: 200 us
  waiting for transfers between devices  87.3 us (43%)
  Pallas kernels  56.6 us (28%)
  starting transfers between devices  41.7 us (21%)
  local copies, waits for them, and re-layouts  10.3 us (5%)
  matrix products  3.4 us (2%)
    all_to_all x2, waiting for transfers between devices, layer(): lax.all_to_all(outgoing.reshape(experts, part_cap, D), ('node', 'expert')...  35.7 us
    pallas_call x2, Pallas kernels, run_expert(): pl.pallas_call(expert_kernel, out_shape=jax.ShapeDtypeStruct((count, D),...  29.5 us
    all_to_all x2, waiting for transfers between devices, layer(): lax.all_to_all(result.reshape(block.shape), ('node', 'expert'), split_axi...  28.1 us
    pallas_call x8, Pallas kernels, attend(): pl.pallas_call(lambda *refs: attend_kernel(sizes, *refs), out_shape=jax.S...  17.9 us
    ppermute x8, waiting for transfers between devices, layer(): near = lax.ppermute(own, 'node', swap)  17.7 us
    ppermute x8, starting transfers between devices, layer(): near = lax.ppermute(own, 'node', swap)  12.9 us
    ppermute x8, starting transfers between devices, layer(): far = lax.ppermute(near, 'node', onward)  12.4 us
    all_to_all x2, starting transfers between devices, layer(): lax.all_to_all(outgoing.reshape(experts, part_cap, D), ('node', 'expert')...  9.15 us
  transfers between devices with their start and end apart: 20, of which 12 were waited for; matrix products, arithmetic and copies ran while one was open for 4% of the time, Pallas kernels for 24%

profile of v3, /device:TPU:0, one launch (start us, length us, event | category | flops | bytes accessed | tf_op | source)
XLA Modules:
  0.0 199.9 jit_solution(5624811832158653718)
XLA Ops:
  1.8 3.0 %collective-permute-start = (bf16[1024,128]{1,0:T(8,128)(2,1)}, bf16[1024,128]{1,0:T(8,128)(2,1)S(1)}, u32[]{:S(2)}, u32[]{:S(2)}) collective-permute-start(bf16[1024,128]{1,0:T(8,128)(2,1)} %pack.2), channel_id=1, source_target_pairs={{0,4},{4,0},{8,12},{12,8},{16,20},{20,16},{24,28},{28,24},{1,5},{5... | collective-permute-start | bytes 786440 | tf_op jit(solution)/shard_map/ppermute | solution.py:394
  4.8 2.9 %pack.3 = (bf16[1024,128]{1,0:T(8,128)(2,1)}, bf16[1024,128]{1,0:T(8,128)(2,1)}, bf16[1024,128]{1,0:T(8,128)(2,1)}, bf16[1024,128]{1,0:T(8,128)(2,1)}, bf16[1024...) custom-call(bf16[512,1024]{1,0:T(8,128)(2,1)} %refs_0_.3, bf16[512,1024]{1,0:T(8,128)(2,1)} %refs_1_.12), custom_call_target="tpu_custom_call" | custom-call | tf_op jit(solution)/shard_map/pack/pallas_call | solution.py:35
  7.7 2.0 collective-permute-start.4
  9.8 2.0 collective-permute-start.8
  12.2 2.0 %collective-permute-start.1 = (bf16[1024,128]{1,0:T(8,128)(2,1)S(1)}, bf16[1024,128]{1,0:T(8,128)(2,1)S(1)}, u32[]{:S(2)}, u32[]{:S(2)}) collective-permute-start(bf16[1024,128]{1,0:T(8,128)(2,1)S(1)} %collective-permute-done), channel_id=1, source_target_pairs={{0,8},{4,28},{8,16},{12,4},{16,24},{20,12},{24,0},{28,20},{1,9},{5... | collective-permute-start | bytes 786440 | tf_op jit(solution)/shard_map/ppermute | solution.py:395
  14.3 3.6 %collective-permute-done.2 = bf16[1024,128]{1,0:T(8,128)(2,1)S(1)} collective-permute-done((bf16[1024,128]{1,0:T(8,128)(2,1)}, bf16[1024,128]{1,0:T(8,128)(2,1)S(1)}, u32[]{:S(2)}, u32[]{:S(2)}) %collective-permute-start.2) | collective-permute-done | bytes 262176 | tf_op jit(solution)/shard_map/ppermute | solution.py:394
  17.8 2.0 %collective-permute-start.3 = (bf16[1024,128]{1,0:T(8,128)(2,1)S(1)}, bf16[1024,128]{1,0:T(8,128)(2,1)S(1)}, u32[]{:S(2)}, u32[]{:S(2)}) collective-permute-start(bf16[1024,128]{1,0:T(8,128)(2,1)S(1)} %collective-permute-done.2), channel_id=1, source_target_pairs={{0,8},{4,28},{8,16},{12,4},{16,24},{20,12},{24,0},{28,20},{1,9},{5... | collective-permute-start | bytes 786440 | tf_op jit(solution)/shard_map/ppermute | solution.py:395
  19.9 3.6 %collective-permute-done.4 = bf16[1024,128]{1,0:T(8,128)(2,1)S(1)} collective-permute-done((bf16[1024,128]{1,0:T(8,128)(2,1)}, bf16[1024,128]{1,0:T(8,128)(2,1)S(1)}, u32[]{:S(2)}, u32[]{:S(2)}) %collective-permute-start.4) | collective-permute-done | bytes 262176 | tf_op jit(solution)/shard_map/ppermute | solution.py:394
  25.4 3.7 %collective-permute-done.6 = bf16[1024,128]{1,0:T(8,128)(2,1)S(1)} collective-permute-done((bf16[1024,128]{1,0:T(8,128)(2,1)}, bf16[1024,128]{1,0:T(8,128)(2,1)S(1)}, u32[]{:S(2)}, u32[]{:S(2)}) %collective-permute-start.6) | collective-permute-done | bytes 262176 | tf_op jit(solution)/shard_map/ppermute | solution.py:394
  31.0 3.7 %collective-permute-done.8 = bf16[1024,128]{1,0:T(8,128)(2,1)S(1)} collective-permute-done((bf16[1024,128]{1,0:T(8,128)(2,1)}, bf16[1024,128]{1,0:T(8,128)(2,1)S(1)}, u32[]{:S(2)}, u32[]{:S(2)}) %collective-permute-start.8) | collective-permute-done | bytes 262176 | tf_op jit(solution)/shard_map/ppermute | solution.py:394
  41.6 2.3 %attend.8 = bf16[512,128]{1,0:T(8,128)(2,1)S(1)} custom-call(s32[4,8]{1,0:T(4,128)S(1)} %fusion.10.refs_0_, s32[4,8]{1,0:T(4,128)S(1)} %copy-done.19, bf16[512,1024]{1,0:T(8,128)(2,1)S(1)} %copy-done.9, bf16[8,128,128]{2,1,0:T(8,128)(2,1)S(1)} %bitcast.45, bf16[8,128,128]{2,1,0:T(8,128)(2,1)S(1)} %bitcast.59, bf16[8,128,128]{2,1,0:T(8,128)(2,1)S(1)} %bitcast.64), custom_call_target="tpu_custom_call" | custom-call | flops 536870912 | bytes 1048576 | tf_op jit(solution)/shard_map/attend/pallas_call | solution.py:156
  43.9 2.2 %attend.9 = bf16[512,128]{1,0:T(8,128)(2,1)S(1)} custom-call(s32[4,8]{1,0:T(4,128)S(1)} %fusion.10.refs_0_, s32[4,8]{1,0:T(4,128)S(1)} %copy-done.19, bf16[512,1024]{1,0:T(8,128)(2,1)S(1)} %copy-done.9, bf16[8,128,128]{2,1,0:T(8,128)(2,1)S(1)} %bitcast.58, bf16[8,128,128]{2,1,0:T(8,128)(2,1)S(1)} %bitcast.60, bf16[8,128,128]{2,1,0:T(8,128)(2,1)S(1)} %bitcast.65), custom_call_target="tpu_custom_call" | custom-call | flops 536870912 | bytes 1048576 | tf_op jit(solution)/shard_map/attend/pallas_call | solution.py:156
  48.0 2.7 %collective-permute-done.14 = bf16[1024,128]{1,0:T(8,128)(2,1)S(1)} collective-permute-done((bf16[1024,128]{1,0:T(8,128)(2,1)}, bf16[1024,128]{1,0:T(8,128)(2,1)S(1)}, u32[]{:S(2)}, u32[]{:S(2)}) %collective-permute-start.14) | collective-permute-done | bytes 262176 | tf_op jit(solution)/shard_map/ppermute | solution.py:394
  54.0 2.2 %attend.10 = bf16[512,128]{1,0:T(8,128)(2,1)S(1)} custom-call(s32[4,8]{1,0:T(4,128)S(1)} %fusion.10.refs_0_, s32[4,8]{1,0:T(4,128)S(1)} %copy-done.19, bf16[512,1024]{1,0:T(8,128)(2,1)S(1)} %copy-done.9, bf16[8,128,128]{2,1,0:T(8,128)(2,1)S(1)} %bitcast.54, bf16[8,128,128]{2,1,0:T(8,128)(2,1)S(1)} %bitcast.57, bf16[8,128,128]{2,1,0:T(8,128)(2,1)S(1)} %bitcast.68), custom_call_target="tpu_custom_call" | custom-call | flops 536870912 | bytes 1048576 | tf_op jit(solution)/shard_map/attend/pallas_call | solution.py:156
  56.3 2.2 %attend.11 = bf16[512,128]{1,0:T(8,128)(2,1)S(1)} custom-call(s32[4,8]{1,0:T(4,128)S(1)} %fusion.10.refs_0_, s32[4,8]{1,0:T(4,128)S(1)} %copy-done.19, bf16[512,1024]{1,0:T(8,128)(2,1)S(1)} %copy-done.9, bf16[8,128,128]{2,1,0:T(8,128)(2,1)S(1)} %bitcast.53, bf16[8,128,128]{2,1,0:T(8,128)(2,1)S(1)} %bitcast.56, bf16[8,128,128]{2,1,0:T(8,128)(2,1)S(1)} %bitcast.69), custom_call_target="tpu_custom_call" | custom-call | flops 536870912 | bytes 1048576 | tf_op jit(solution)/shard_map/attend/pallas_call | solution.py:156
  58.7 2.2 %attend.12 = bf16[512,128]{1,0:T(8,128)(2,1)S(1)} custom-call(s32[4,8]{1,0:T(4,128)S(1)} %fusion.10.refs_0_, s32[4,8]{1,0:T(4,128)S(1)} %copy-done.19, bf16[512,1024]{1,0:T(8,128)(2,1)S(1)} %copy-done.9, bf16[8,128,128]{2,1,0:T(8,128)(2,1)S(1)} %bitcast.52, bf16[8,128,128]{2,1,0:T(8,128)(2,1)S(1)} %bitcast.55, bf16[8,128,128]{2,1,0:T(8,128)(2,1)S(1)} %bitcast.71), custom_call_target="tpu_custom_call" | custom-call | flops 536870912 | bytes 1048576 | tf_op jit(solution)/shard_map/attend/pallas_call | solution.py:156
  61.0 2.5 %collective-permute-done.11 = bf16[1024,128]{1,0:T(8,128)(2,1)S(1)} collective-permute-done((bf16[1024,128]{1,0:T(8,128)(2,1)S(1)}, bf16[1024,128]{1,0:T(8,128)(2,1)S(1)}, u32[]{:S(2)}, u32[]{:S(2)}) %collective-permute-start.11) | collective-permute-done | bytes 262176 | tf_op jit(solution)/shard_map/ppermute | solution.py:395
  63.5 2.2 %attend.13 = bf16[512,128]{1,0:T(8,128)(2,1)S(1)} custom-call(s32[4,8]{1,0:T(4,128)S(1)} %fusion.10.refs_0_, s32[4,8]{1,0:T(4,128)S(1)} %copy-done.19, bf16[512,1024]{1,0:T(8,128)(2,1)S(1)} %copy-done.9, bf16[8,128,128]{2,1,0:T(8,128)(2,1)S(1)} %bitcast.51, bf16[8,128,128]{2,1,0:T(8,128)(2,1)S(1)} %bitcast.63, bf16[8,128,128]{2,1,0:T(8,128)(2,1)S(1)} %bitcast.70), custom_call_target="tpu_custom_call" | custom-call | flops 536870912 | bytes 1048576 | tf_op jit(solution)/shard_map/attend/pallas_call | solution.py:156
  65.8 3.3 %collective-permute-done.13 = bf16[1024,128]{1,0:T(8,128)(2,1)S(1)} collective-permute-done((bf16[1024,128]{1,0:T(8,128)(2,1)S(1)}, bf16[1024,128]{1,0:T(8,128)(2,1)S(1)}, u32[]{:S(2)}, u32[]{:S(2)}) %collective-permute-start.13) | collective-permute-done | bytes 262176 | tf_op jit(solution)/shard_map/ppermute | solution.py:395
  69.1 2.2 %attend.14 = bf16[512,128]{1,0:T(8,128)(2,1)S(1)} custom-call(s32[4,8]{1,0:T(4,128)S(1)} %fusion.10.refs_0_, s32[4,8]{1,0:T(4,128)S(1)} %copy-done.19, bf16[512,1024]{1,0:T(8,128)(2,1)S(1)} %copy-done.9, bf16[8,128,128]{2,1,0:T(8,128)(2,1)S(1)} %bitcast.50, bf16[8,128,128]{2,1,0:T(8,128)(2,1)S(1)} %bitcast.62, bf16[8,128,128]{2,1,0:T(8,128)(2,1)S(1)} %bitcast.67), custom_call_target="tpu_custom_call" | custom-call | flops 536870912 | bytes 1048576 | tf_op jit(solution)/shard_map/attend/pallas_call | solution.py:156
  72.7 2.2 %attend.15.refs_0_ = bf16[512,128]{1,0:T(8,128)(2,1)S(1)} custom-call(s32[4,8]{1,0:T(4,128)S(1)} %fusion.10.refs_0_, s32[4,8]{1,0:T(4,128)S(1)} %copy-done.19, bf16[512,1024]{1,0:T(8,128)(2,1)S(1)} %copy-done.9, bf16[8,128,128]{2,1,0:T(8,128)(2,1)S(1)} %bitcast.49, bf16[8,128,128]{2,1,0:T(8,128)(2,1)S(1)} %bitcast.61, bf16[8,128,128]{2,1,0:T(8,128)(2,1)S(1)} %bitcast.66), custom_call_target="tpu_custom_call" | custom-call | flops 536870912 | bytes 1048576 | tf_op jit(solution)/shard_map/attend/pallas_call | solution.py:156
  75.0 2.1 %norm.1 = (f32[512,1024]{1,0:T(8,128)}, bf16[512,1024]{1,0:T(8,128)(2,1)S(1)}, bf16[512,1024]{1,0:T(8,128)(2,1)}) custom-call(f32[512,1024]{1,0:T(8,128)S(1)} %convert_add_fusion.pre_ref, bf16[512,128]{1,0:T(8,128)(2,1)S(1)} %attend.15.refs_0_, bf16[128,1024]{1,0:T(8,128)(2,1)S(1)} %slice.7.refs_1_, f32[1,1024]{1,0:T(1,128)S(1)} %bitcast.48, ...), custom_call_target="tpu_custom_call" | custom-call | tf_op jit(solution)/shard_map/norm/pallas_call | solution.py:223
  77.1 5.3 %all-to-all-start = ((bf16[32,16,1024]{2,1,0:T(8,128)(2,1)}), bf16[32,16,1024]{2,1,0:T(8,128)(2,1)S(1)}, u32[]{:S(2)}, u32[]{:S(2)}) async-start(bf16[32,16,1024]{2,1,0:T(8,128)(2,1)} %bitcast.75), calls=%async_computation | async-start | bytes 2097152 | tf_op jit(solution)/shard_map/all_to_all | solution.py:426
  84.1 24.5 %all-to-all-done = bf16[32,16,1024]{2,1,0:T(8,128)(2,1)S(1)} async-done(((bf16[32,16,1024]{2,1,0:T(8,128)(2,1)}), bf16[32,16,1024]{2,1,0:T(8,128)(2,1)S(1)}, u32[]{:S(2)}, u32[]{:S(2)}) %all-to-all-start) | async-done | bytes 1048608 | tf_op jit(solution)/shard_map/all_to_all | solution.py:426
  108.7 3.8 %all-to-all-start.2 = ((bf16[32,16,1024]{2,1,0:T(8,128)(2,1)}), bf16[32,16,1024]{2,1,0:T(8,128)(2,1)S(1)}, u32[]{:S(2)}, u32[]{:S(2)}) async-start(bf16[32,16,1024]{2,1,0:T(8,128)(2,1)} %bitcast.77), calls=%async_computation.2 | async-start | bytes 2097152 | tf_op jit(solution)/shard_map/all_to_all | solution.py:426
  112.5 14.8 %expert.2 = bf16[512,1024]{1,0:T(8,128)(2,1)} custom-call(bf16[512,1024]{1,0:T(8,128)(2,1)} %bitcast.73, bf16[1024,4096]{1,0:T(8,128)(2,1)} %bitcast.80, bf16[4096,1024]{1,0:T(8,128)(2,1)} %bitcast.82), custom_call_target="tpu_custom_call" | custom-call | flops 8589934592 | bytes 16777216 | tf_op jit(solution)/shard_map/expert/pallas_call | solution.py:337
  127.3 11.2 %all-to-all-done.2 = bf16[32,16,1024]{2,1,0:T(8,128)(2,1)S(1)} async-done(((bf16[32,16,1024]{2,1,0:T(8,128)(2,1)}), bf16[32,16,1024]{2,1,0:T(8,128)(2,1)S(1)}, u32[]{:S(2)}, u32[]{:S(2)}) %all-to-all-start.2) | async-done | bytes 1048608 | tf_op jit(solution)/shard_map/all_to_all | solution.py:426
  138.5 3.6 %all-to-all-start.1 = ((bf16[32,16,1024]{2,1,0:T(8,128)(2,1)}), bf16[32,16,1024]{2,1,0:T(8,128)(2,1)S(1)}, u32[]{:S(2)}, u32[]{:S(2)}) async-start(bf16[32,16,1024]{2,1,0:T(8,128)(2,1)} %bitcast.76), calls=%async_computation.1 | async-start | bytes 2097152 | tf_op jit(solution)/shard_map/all_to_all | solution.py:434
  142.1 14.8 %expert.3 = bf16[512,1024]{1,0:T(8,128)(2,1)} custom-call(bf16[512,1024]{1,0:T(8,128)(2,1)} %bitcast.74, bf16[1024,4096]{1,0:T(8,128)(2,1)} %bitcast.81, bf16[4096,1024]{1,0:T(8,128)(2,1)} %bitcast.83), custom_call_target="tpu_custom_call" | custom-call | flops 8589934592 | bytes 16777216 | tf_op jit(solution)/shard_map/expert/pallas_call | solution.py:337
  156.9 11.4 %all-to-all-done.1 = bf16[32,16,1024]{2,1,0:T(8,128)(2,1)S(1)} async-done(((bf16[32,16,1024]{2,1,0:T(8,128)(2,1)}), bf16[32,16,1024]{2,1,0:T(8,128)(2,1)S(1)}, u32[]{:S(2)}, u32[]{:S(2)}) %all-to-all-start.1) | async-done | bytes 1048608 | tf_op jit(solution)/shard_map/all_to_all | solution.py:434
  168.3 3.6 %all-to-all-start.3 = ((bf16[32,16,1024]{2,1,0:T(8,128)(2,1)}), bf16[32,16,1024]{2,1,0:T(8,128)(2,1)S(1)}, u32[]{:S(2)}, u32[]{:S(2)}) async-start(bf16[32,16,1024]{2,1,0:T(8,128)(2,1)} %bitcast.72), calls=%async_computation.3 | async-start | bytes 2097152 | tf_op jit(solution)/shard_map/all_to_all | solution.py:434
  181.5 16.7 %all-to-all-done.3 = bf16[32,16,1024]{2,1,0:T(8,128)(2,1)S(1)} async-done(((bf16[32,16,1024]{2,1,0:T(8,128)(2,1)}), bf16[32,16,1024]{2,1,0:T(8,128)(2,1)S(1)}, u32[]{:S(2)}, u32[]{:S(2)}) %all-to-all-start.3) | async-done | bytes 1048608 | tf_op jit(solution)/shard_map/all_to_all | solution.py:434
  (94 shorter events, 32.6 us)
Async XLA Ops:
  0.0 173.7 %copy-start = (bf16[1024,32]{0,1:T(8,128)(2,1)S(1)}, bf16[1024,32]{0,1:T(8,128)(2,1)}, u32[]{:S(2)}) copy-start(bf16[1024,32]{0,1:T(8,128)(2,1)} %param.21) | copy-start | bytes 196612
  0.0 19.9 %copy-start.23 = (s32[512]{0:T(512)S(1)}, s32[512]{0:T(512)}, u32[]{:S(2)}) copy-start(s32[512]{0:T(512)} %param.22) | copy-start | bytes 6148
  0.0 19.9 %copy-start.25 = (s32[512]{0:T(512)S(1)}, s32[512]{0:T(512)}, u32[]{:S(2)}) copy-start(s32[512]{0:T(512)} %param.23) | copy-start | bytes 6148
  0.0 40.5 %copy-start.24 = (s32[4,8]{1,0:T(4,128)S(1)}, s32[4,8]{1,0:T(4,128)}, u32[]{:S(2)}) copy-start(s32[4,8]{1,0:T(4,128)} %param.17) | copy-start | bytes 388
  0.0 41.6 %copy-start.19 = (s32[4,8]{1,0:T(4,128)S(1)}, s32[4,8]{1,0:T(4,128)}, u32[]{:S(2)}) copy-start(s32[4,8]{1,0:T(4,128)} %refs_1_.19) | copy-start | bytes 388
  0.0 41.6 %copy-start.9 = (bf16[512,1024]{1,0:T(8,128)(2,1)S(1)}, bf16[512,1024]{1,0:T(8,128)(2,1)}, u32[]{:S(2)}) copy-start(bf16[512,1024]{1,0:T(8,128)(2,1)} %refs_2_.15) | copy-start | bytes 3145732
  1.8 39.8 %copy-start.7 = (bf16[1024,128]{1,0:T(8,128)(2,1)S(1)}, bf16[1024,128]{1,0:T(8,128)(2,1)}, u32[]{:S(2)}) copy-start(bf16[1024,128]{1,0:T(8,128)(2,1)} %pack.2) | copy-start | bytes 786436
  1.8 10.4 %collective-permute-start = (bf16[1024,128]{1,0:T(8,128)(2,1)}, bf16[1024,128]{1,0:T(8,128)(2,1)S(1)}, u32[]{:S(2)}, u32[]{:S(2)}) collective-permute-start(bf16[1024,128]{1,0:T(8,128)(2,1)} %pack.2), channel_id=1, source_target_pairs={{0,4},{4,0},{8,12},{12,8},{16,20},{20,16},{24,28},{28,24},{1,5},{5... | collective-permute-start | bytes 786440 | tf_op jit(solution)/shard_map/ppermute | solution.py:394
  7.7 36.2 %copy-start.16 = (bf16[1024,128]{1,0:T(8,128)(2,1)S(1)}, bf16[1024,128]{1,0:T(8,128)(2,1)}, u32[]{:S(2)}) copy-start(bf16[1024,128]{1,0:T(8,128)(2,1)} %get-tuple-element.15) | copy-start | bytes 786436
  7.7 10.2 %collective-permute-start.2 = (bf16[1024,128]{1,0:T(8,128)(2,1)}, bf16[1024,128]{1,0:T(8,128)(2,1)S(1)}, u32[]{:S(2)}, u32[]{:S(2)}) collective-permute-start(bf16[1024,128]{1,0:T(8,128)(2,1)} %get-tuple-element.15), channel_id=1, source_target_pairs={{0,4},{4,0},{8,12},{12,8},{16,20},{20,16},{24,28},{28,24},{1,5},{5... | collective-permute-start | bytes 786440 | tf_op jit(solution)/shard_map/ppermute | solution.py:394
  7.7 15.7 %collective-permute-start.4 = (bf16[1024,128]{1,0:T(8,128)(2,1)}, bf16[1024,128]{1,0:T(8,128)(2,1)S(1)}, u32[]{:S(2)}, u32[]{:S(2)}) collective-permute-start(bf16[1024,128]{1,0:T(8,128)(2,1)} %get-tuple-element.16), channel_id=1, source_target_pairs={{0,4},{4,0},{8,12},{12,8},{16,20},{20,16},{24,28},{28,24},{1,5},{5... | collective-permute-start | bytes 786440 | tf_op jit(solution)/shard_map/ppermute | solution.py:394
  9.7 19.4 %collective-permute-start.6 = (bf16[1024,128]{1,0:T(8,128)(2,1)}, bf16[1024,128]{1,0:T(8,128)(2,1)S(1)}, u32[]{:S(2)}, u32[]{:S(2)}) collective-permute-start(bf16[1024,128]{1,0:T(8,128)(2,1)} %get-tuple-element.17), channel_id=1, source_target_pairs={{0,4},{4,0},{8,12},{12,8},{16,20},{20,16},{24,28},{28,24},{1,5},{5... | collective-permute-start | bytes 786440 | tf_op jit(solution)/shard_map/ppermute | solution.py:394
  9.8 24.9 %collective-permute-start.8 = (bf16[1024,128]{1,0:T(8,128)(2,1)}, bf16[1024,128]{1,0:T(8,128)(2,1)S(1)}, u32[]{:S(2)}, u32[]{:S(2)}) collective-permute-start(bf16[1024,128]{1,0:T(8,128)(2,1)} %get-tuple-element.18), channel_id=1, source_target_pairs={{0,4},{4,0},{8,12},{12,8},{16,20},{20,16},{24,28},{28,24},{1,5},{5... | collective-permute-start | bytes 786440 | tf_op jit(solution)/shard_map/ppermute | solution.py:394
  12.2 24.4 %collective-permute-start.1 = (bf16[1024,128]{1,0:T(8,128)(2,1)S(1)}, bf16[1024,128]{1,0:T(8,128)(2,1)S(1)}, u32[]{:S(2)}, u32[]{:S(2)}) collective-permute-start(bf16[1024,128]{1,0:T(8,128)(2,1)S(1)} %collective-permute-done), channel_id=1, source_target_pairs={{0,8},{4,28},{8,16},{12,4},{16,24},{20,12},{24,0},{28,20},{1,9},{5... | collective-permute-start | bytes 786440 | tf_op jit(solution)/shard_map/ppermute | solution.py:395
  17.8 20.4 %collective-permute-start.3 = (bf16[1024,128]{1,0:T(8,128)(2,1)S(1)}, bf16[1024,128]{1,0:T(8,128)(2,1)S(1)}, u32[]{:S(2)}, u32[]{:S(2)}) collective-permute-start(bf16[1024,128]{1,0:T(8,128)(2,1)S(1)} %collective-permute-done.2), channel_id=1, source_target_pairs={{0,8},{4,28},{8,16},{12,4},{16,24},{20,12},{24,0},{28,20},{1,9},{5... | collective-permute-start | bytes 786440 | tf_op jit(solution)/shard_map/ppermute | solution.py:395
  23.5 22.7 %collective-permute-start.10 = (bf16[1024,128]{1,0:T(8,128)(2,1)}, bf16[1024,128]{1,0:T(8,128)(2,1)S(1)}, u32[]{:S(2)}, u32[]{:S(2)}) collective-permute-start(bf16[1024,128]{1,0:T(8,128)(2,1)} %get-tuple-element.19), channel_id=1, source_target_pairs={{0,4},{4,0},{8,12},{12,8},{16,20},{20,16},{24,28},{28,24},{1,5},{5... | collective-permute-start | bytes 786440 | tf_op jit(solution)/shard_map/ppermute | solution.py:394
  29.1 18.7 %collective-permute-start.12 = (bf16[1024,128]{1,0:T(8,128)(2,1)}, bf16[1024,128]{1,0:T(8,128)(2,1)S(1)}, u32[]{:S(2)}, u32[]{:S(2)}) collective-permute-start(bf16[1024,128]{1,0:T(8,128)(2,1)} %get-tuple-element.20), channel_id=1, source_target_pairs={{0,4},{4,0},{8,12},{12,8},{16,20},{20,16},{24,28},{28,24},{1,5},{5... | collective-permute-start | bytes 786440 | tf_op jit(solution)/shard_map/ppermute | solution.py:394
  34.7 16.0 %collective-permute-start.14 = (bf16[1024,128]{1,0:T(8,128)(2,1)}, bf16[1024,128]{1,0:T(8,128)(2,1)S(1)}, u32[]{:S(2)}, u32[]{:S(2)}) collective-permute-start(bf16[1024,128]{1,0:T(8,128)(2,1)} %get-tuple-element.21), channel_id=1, source_target_pairs={{0,4},{4,0},{8,12},{12,8},{16,20},{20,16},{24,28},{28,24},{1,5},{5... | collective-permute-start | bytes 786440 | tf_op jit(solution)/shard_map/ppermute | solution.py:394
  36.7 15.8 %collective-permute-start.5 = (bf16[1024,128]{1,0:T(8,128)(2,1)S(1)}, bf16[1024,128]{1,0:T(8,128)(2,1)S(1)}, u32[]{:S(2)}, u32[]{:S(2)}) collective-permute-start(bf16[1024,128]{1,0:T(8,128)(2,1)S(1)} %collective-permute-done.4), channel_id=1, source_target_pairs={{0,8},{4,28},{8,16},{12,4},{16,24},{20,12},{24,0},{28,20},{1,9},{5... | collective-permute-start | bytes 786440 | tf_op jit(solution)/shard_map/ppermute | solution.py:395
  38.9 17.4 %collective-permute-start.7 = (bf16[1024,128]{1,0:T(8,128)(2,1)S(1)}, bf16[1024,128]{1,0:T(8,128)(2,1)S(1)}, u32[]{:S(2)}, u32[]{:S(2)}) collective-permute-start(bf16[1024,128]{1,0:T(8,128)(2,1)S(1)} %collective-permute-done.6), channel_id=1, source_target_pairs={{0,8},{4,28},{8,16},{12,4},{16,24},{20,12},{24,0},{28,20},{1,9},{5... | collective-permute-start | bytes 786440 | tf_op jit(solution)/shard_map/ppermute | solution.py:395
  41.6 12.5 %copy-start.15 = (bf16[1024,128]{1,0:T(8,128)(2,1)S(1)}, bf16[1024,128]{1,0:T(8,128)(2,1)}, u32[]{:S(2)}) copy-start(bf16[1024,128]{1,0:T(8,128)(2,1)} %get-tuple-element.16) | copy-start | bytes 786436
  43.9 12.4 %copy-start.14 = (bf16[1024,128]{1,0:T(8,128)(2,1)S(1)}, bf16[1024,128]{1,0:T(8,128)(2,1)}, u32[]{:S(2)}) copy-start(bf16[1024,128]{1,0:T(8,128)(2,1)} %get-tuple-element.17) | copy-start | bytes 786436
  46.1 12.5 %collective-permute-start.9 = (bf16[1024,128]{1,0:T(8,128)(2,1)S(1)}, bf16[1024,128]{1,0:T(8,128)(2,1)S(1)}, u32[]{:S(2)}, u32[]{:S(2)}) collective-permute-start(bf16[1024,128]{1,0:T(8,128)(2,1)S(1)} %collective-permute-done.8), channel_id=1, source_target_pairs={{0,8},{4,28},{8,16},{12,4},{16,24},{20,12},{24,0},{28,20},{1,9},{5... | collective-permute-start | bytes 786440 | tf_op jit(solution)/shard_map/ppermute | solution.py:395
  47.8 15.7 %collective-permute-start.11 = (bf16[1024,128]{1,0:T(8,128)(2,1)S(1)}, bf16[1024,128]{1,0:T(8,128)(2,1)S(1)}, u32[]{:S(2)}, u32[]{:S(2)}) collective-permute-start(bf16[1024,128]{1,0:T(8,128)(2,1)S(1)} %collective-permute-done.10), channel_id=1, source_target_pairs={{0,8},{4,28},{8,16},{12,4},{16,24},{20,12},{24,0},{28,20},{1,9},{5... | collective-permute-start | bytes 786440 | tf_op jit(solution)/shard_map/ppermute | solution.py:395
  50.7 18.4 %collective-permute-start.13 = (bf16[1024,128]{1,0:T(8,128)(2,1)S(1)}, bf16[1024,128]{1,0:T(8,128)(2,1)S(1)}, u32[]{:S(2)}, u32[]{:S(2)}) collective-permute-start(bf16[1024,128]{1,0:T(8,128)(2,1)S(1)} %collective-permute-done.12), channel_id=1, source_target_pairs={{0,8},{4,28},{8,16},{12,4},{16,24},{20,12},{24,0},{28,20},{1,9},{5... | collective-permute-start | bytes 786440 | tf_op jit(solution)/shard_map/ppermute | solution.py:395
  52.5 20.3 %collective-permute-start.15 = (bf16[1024,128]{1,0:T(8,128)(2,1)S(1)}, bf16[1024,128]{1,0:T(8,128)(2,1)S(1)}, u32[]{:S(2)}, u32[]{:S(2)}) collective-permute-start(bf16[1024,128]{1,0:T(8,128)(2,1)S(1)} %collective-permute-done.14), channel_id=1, source_target_pairs={{0,8},{4,28},{8,16},{12,4},{16,24},{20,12},{24,0},{28,20},{1,9},{5... | collective-permute-start | bytes 786440 | tf_op jit(solution)/shard_map/ppermute | solution.py:395
  58.7 10.4 %copy-start.11 = (bf16[1024,128]{1,0:T(8,128)(2,1)S(1)}, bf16[1024,128]{1,0:T(8,128)(2,1)}, u32[]{:S(2)}) copy-start(bf16[1024,128]{1,0:T(8,128)(2,1)} %get-tuple-element.20) | copy-start | bytes 786436
  63.5 7.9 %copy-start.26 = (bf16[512,1024]{1,0:T(8,128)(2,1)S(1)}, bf16[512,1024]{1,0:T(8,128)(2,1)}, u32[]{:S(2)}) copy-start(bf16[512,1024]{1,0:T(8,128)(2,1)} %param.13) | copy-start | bytes 3145732
  77.1 31.5 %all-to-all-start = ((bf16[32,16,1024]{2,1,0:T(8,128)(2,1)}), bf16[32,16,1024]{2,1,0:T(8,128)(2,1)S(1)}, u32[]{:S(2)}, u32[]{:S(2)}) async-start(bf16[32,16,1024]{2,1,0:T(8,128)(2,1)} %bitcast.75), calls=%async_computation | async-start | bytes 2097152 | tf_op jit(solution)/shard_map/all_to_all | solution.py:426
  108.7 29.8 %all-to-all-start.2 = ((bf16[32,16,1024]{2,1,0:T(8,128)(2,1)}), bf16[32,16,1024]{2,1,0:T(8,128)(2,1)S(1)}, u32[]{:S(2)}, u32[]{:S(2)}) async-start(bf16[32,16,1024]{2,1,0:T(8,128)(2,1)} %bitcast.77), calls=%async_computation.2 | async-start | bytes 2097152 | tf_op jit(solution)/shard_map/all_to_all | solution.py:426
  138.5 29.8 %all-to-all-start.1 = ((bf16[32,16,1024]{2,1,0:T(8,128)(2,1)}), bf16[32,16,1024]{2,1,0:T(8,128)(2,1)S(1)}, u32[]{:S(2)}, u32[]{:S(2)}) async-start(bf16[32,16,1024]{2,1,0:T(8,128)(2,1)} %bitcast.76), calls=%async_computation.1 | async-start | bytes 2097152 | tf_op jit(solution)/shard_map/all_to_all | solution.py:434
  168.3 29.8 %all-to-all-start.3 = ((bf16[32,16,1024]{2,1,0:T(8,128)(2,1)}), bf16[32,16,1024]{2,1,0:T(8,128)(2,1)S(1)}, u32[]{:S(2)}, u32[]{:S(2)}) async-start(bf16[32,16,1024]{2,1,0:T(8,128)(2,1)} %bitcast.72), calls=%async_computation.3 | async-start | bytes 2097152 | tf_op jit(solution)/shard_map/all_to_all | solution.py:434
  (15 other events, 48.5 us)
